TPU v7x, 32 devices: a whole 2x2x4 slice. The times are simulated.
32 devices in a mesh: ang: 4 (over y, x), rad: 8 (over z, core).
Axes of the slice: x: 2, y: 2, z: 4, core: 2. Of those that a mesh axis runs over, the one named last changes fastest.
Arguments:
- right_side: float32 [1024, 4096], P('rad', 'ang'), may hold values from -6 to 7
- guess: float32 [1024, 4096], P('rad', 'ang'), may hold values from -6 to 6
Outputs:
- solution: float32 [1024, 4096], P('rad', 'ang')
- residual: float32 [1024, 4096], P('rad', 'ang')
All inputs are finite; a program needn't handle non-finite values.
Results may differ from a plain program's by a relative error of at most 0.007.
Values sent between devices are 32-bit elements; how exact they have to be, the bound alone decides.
A program may use at most 128 MiB of HBM per device.

v0:
```python
import math

import jax
import jax.numpy as jnp
from jax import lax
from jax.experimental import pallas as pl
from jax.experimental.pallas import tpu as pltpu
from jax.sharding import PartitionSpec as P

LEVELS = 8
PRE = 2
POST = 2
COARSE_SWEEPS = 8
F32 = jnp.float32
MESH = pl.DeviceIdType.MESH
HALO = 16


def one_hot(rows, cols, source):
    r = lax.broadcasted_iota(jnp.int32, (rows, cols), 0)
    c = lax.broadcasted_iota(jnp.int32, (rows, cols), 1)
    return jnp.where(r == source(c), 1.0, 0.0).astype(jnp.bfloat16)


def permute(x, table):
    hi = x.astype(jnp.bfloat16)
    rest = x - hi.astype(F32)
    mid = rest.astype(jnp.bfloat16)
    low = (rest - mid.astype(F32)).astype(jnp.bfloat16)
    n = x.shape[0]
    y = jnp.dot(jnp.concatenate([hi, mid, low], axis=0), table, preferred_element_type=F32)
    return (y[:n] + y[n:2 * n]) + y[2 * n:]


def wide(c, lanes):
    return jnp.concatenate([c] * (lanes // c.shape[1]), axis=1) if lanes > c.shape[1] else c


def roll(x, shift, axis):
    return pltpu.roll(x, shift % x.shape[axis], axis)


class Grid:
    def __init__(self, v, g, c, nr, nc, closed):
        self.v, self.g, self.c, self.nr, self.nc, self.closed = v, g, c, nr, nc, closed

    def rows_shift(self, x, d):
        y = roll(x, -d, 0)
        if self.closed:
            s = lax.broadcasted_iota(jnp.int32, x.shape, 0)
            y = jnp.where(s == (x.shape[0] - 1 if d > 0 else 0), 0.0, y)
        return y

    def up(self, a, gi, gj):
        return a[gi + 1, gj] if gi + 1 < self.nr else self.rows_shift(a[0, gj], 1)

    def down(self, a, gi, gj):
        return a[gi - 1, gj] if gi > 0 else self.rows_shift(a[self.nr - 1, gj], -1)

    def right(self, a, gi, gj):
        return a[gi, gj + 1] if gj + 1 < self.nc else roll(a[gi, 0], -1, 1)

    def left(self, a, gi, gj):
        return a[gi, gj - 1] if gj > 0 else roll(a[gi, self.nc - 1], 1, 1)

    def coef(self, k, gi):
        return wide(self.c[k, gi], self.v.shape[-1])

    def update(self, gi, gj):
        v = self.v
        return (self.coef(0, gi) * self.g[gi, gj] + self.coef(1, gi) * self.up(v, gi, gj)
                + self.coef(2, gi) * self.down(v, gi, gj)
                + self.coef(3, gi) * (self.right(v, gi, gj) + self.left(v, gi, gj)))

    def half(self, parity, first=False):
        for gi in range(self.nr):
            for gj in range(self.nc):
                if (gi + gj) % 2 == parity:
                    if first:
                        self.v[gi, gj] = self.coef(0, gi) * self.g[gi, gj]
                    else:
                        self.v[gi, gj] = self.update(gi, gj)

    def sweeps(self, count, zero):
        if zero:
            self.half(0, True)
            self.half(1)
            count -= 1

        def body(_, carry):
            self.half(0)
            self.half(1)
            return carry

        if count:
            lax.fori_loop(0, count, body, 0)

    def restrict(self, res, tmp, out):
        nr, nc = self.nr, self.nc
        for gi in range(nr):
            for gj in range(nc):
                if (gi + gj) % 2 == 0:
                    res[gi, gj] = self.coef(4, gi) * (self.update(gi, gj) - self.v[gi, gj])
        for big in range(nr // 2):
            for gj in range(nc):
                if gj % 2 == 0:
                    a, b = 3.0 * res[2 * big, gj], self.up(res, 2 * big + 1, gj)
                else:
                    a, b = 3.0 * res[2 * big + 1, gj], self.down(res, 2 * big, gj)
                tmp[big, gj] = (a + b) * 0.125
        for big in range(nr // 2):
            for col in range(nc // 2):
                inner = 3.0 * (tmp[big, 2 * col] + tmp[big, 2 * col + 1])
                outer = self.left(tmp, big, 2 * col) + self.right(tmp, big, 2 * col + 1)
                out(big, col, (inner + outer) * 0.5)

    def add_prolonged(self, coarse, tmp, mask, fit=lambda x: x):
        e = coarse.v
        for gi in range(self.nr):
            for col in range(coarse.nc):
                near = e[gi // 2, col]
                far = coarse.down(e, gi // 2, col) if gi % 2 == 0 else coarse.up(e, gi // 2, col)
                value = fit(0.75 * near + 0.25 * far)
                if mask:
                    value = value * self.coef(5, gi)
                tmp[gi, col] = value
        for gi in range(self.nr):
            for gj in range(self.nc):
                near = tmp[gi, gj // 2]
                far = coarse.left(tmp, gi, gj // 2) if gj % 2 == 0 else coarse.right(tmp, gi, gj // 2)
                self.v[gi, gj] = self.v[gi, gj] + (0.75 * near + 0.25 * far)


def fill_coefficients(c, nr, rows_per_group, start, total, spacing, wrap):
    for gi in range(nr):
        s = lax.broadcasted_iota(jnp.int32, (rows_per_group, 128), 0)
        if wrap:
            s = jnp.where(s >= wrap, s - rows_per_group, s)
        row = start + nr * s + gi
        inside = jnp.logical_and(row >= 0, row < total)
        radius = 1.0 + (jnp.where(inside, row, 0).astype(F32) + 0.5) * spacing
        ratio = 0.5 * spacing / radius
        angular = 1.0 / (radius * radius)
        centre = 2.0 + 2.0 * angular
        zero = jnp.zeros_like(radius)
        for k, value in enumerate((1.0 / centre, (1.0 + ratio) / centre, (1.0 - ratio) / centre,
                                   angular / centre, centre, jnp.ones_like(radius))):
            c[k, gi] = jnp.where(inside, value, zero)


def kernel(na, nrad, h, w, rs_in, gs_in, sol, resid, rs, gs, load_sem,
           rowbuf, pack, colbuf, s1, q1, t1, u1, stage, v0, g0, c0, v1, g1, c1, v2, g2, c2, v3, c3, wv, wg, tmp_res, tmp_mid,
           gat, rows3, nat3, a3, b3, d3, a4, b4, d4, a5, b5, d5, a6, b6, d6, a7, b7, d7, t3, u3,
           row_send, row_recv, col_send, col_recv, row1_send, row1_recv, col1_send, col1_recv, all_send, all_recv):
    a, r = lax.axis_index("ang"), lax.axis_index("rad")
    ar, al = lax.rem(a + 1, na), lax.rem(a + na - 1, na)
    lanes = w // 8
    ext = lanes + 128
    tiles = lanes // 128
    spacing = [2.0 * math.pi / (w * na >> l) for l in range(LEVELS)]
    lane = lambda shape: lax.broadcasted_iota(jnp.int32, shape, 1)

    loads = [pltpu.make_async_copy(src, dst, load_sem.at[k]) for k, (src, dst) in enumerate(((gs_in, gs), (rs_in, rs)))]
    for cp in loads:
        cp.start()
    blk = h // 8
    s0 = blk + 8
    total = na * nrad
    barrier = pltpu.get_barrier_semaphore()

    others = sorted(((da, dr) for da in range(na) for dr in range(nrad) if da or dr),
                    key=lambda d: -min(d[1], nrad - d[1]))
    for da, dr in others:
        pl.semaphore_signal(barrier, inc=1, device_id=(lax.rem(a + da, na), lax.rem(r + dr, nrad)), device_id_type=MESH)

    for cp in loads:
        cp.wait()

    fold = h // 4
    place16 = lane((fold, 128)) // 16
    for p, (tile, base) in enumerate(((0, 0), (w - 128, 16))):
        folded = None
        for q in range(4):
            for k, x in enumerate((gs, rs)):
                piece = roll(x[q * fold:(q + 1) * fold, tile:tile + 128], 32 * q + 16 * k + base, 1)
                folded = piece if folded is None else jnp.where(place16 == 2 * q + k, piece, folded)
        pack[p] = folded

    def copy(src, dst, send, recv, to_a, to_r):
        return pltpu.make_async_remote_copy(src_ref=src, dst_ref=dst, send_sem=send, recv_sem=recv,
                                            device_id=(to_a, to_r), device_id_type=MESH)

    def row_copies(side):
        to_r = r - 1 if side == 0 else r + 1
        rows = pl.ds(0, HALO) if side == 0 else pl.ds(h - HALO, HALO)
        made = [copy(x.at[rows, :], rowbuf.at[k, side], row_send.at[k, side], row_recv.at[k, side], a, to_r)
                for k, x in enumerate((gs, rs))]
        for p, to_a in ((0, al), (1, ar)):
            made.append(copy(pack.at[p, pl.ds(side * (fold - HALO), HALO), :], colbuf.at[p, pl.ds(fold + side * HALO, HALO), :],
                             col_send.at[p, 1 + side], col_recv.at[p, 1 + side], to_a, to_r))
        return made

    for l, c in ((0, c0), (1, c1), (2, c2)):
        fill_coefficients(c, 8 >> l, s0 if l == 0 else blk + 16, r * (h >> l), (h * nrad) >> l, spacing[l], blk + 4 if l == 0 else blk + 8)
    for l, d, n in ((3, d3, 16), (4, d4, 8), (5, d5, 4), (6, d6, 2), (7, d7, 1)):
        fill_coefficients(d, n, nrad, 0, (h * nrad) >> l, spacing[l], 0)

    spread = one_hot(256, 256, lambda c: 8 * (c % 32) + c // 32)
    halo_spread = [one_hot(128, 1024, lambda c, k=k: jnp.where(
        c % 128 < 2, 16 * k + 8 * (c % 128) + c // 128,
        jnp.where(c % 128 >= 126, 32 + 16 * k + 8 * (c % 128 - 126) + c // 128, -1))) for k in range(2)]

    def split_rows(x, count, put):
        ln = lane((count, 128)) // 32
        for t in range(tiles):
            parts = [permute(x(slice((4 * t + b) * 256, (4 * t + b) * 256 + 256)), spread) for b in range(4)]
            for gj in range(8):
                o = None
                for b in range(4):
                    half = parts[b][:, (gj // 4) * 128:(gj // 4) * 128 + 128]
                    piece = roll(half, 32 * (b - gj % 4), 1)
                    o = piece if o is None else jnp.where(ln == b, piece, o)
                put(gj, t, o)

    def put_own(k):
        def put(gj, t, value):
            stage[k, gj, t, pl.ds(0, h), :] = value
        return put

    for k, x in enumerate((gs, rs)):
        split_rows(lambda cols, x=x: x[:, cols], h, put_own(k))

    pl.semaphore_wait(barrier, total - 1)
    ends = (r > 0, r < nrad - 1)
    for side in range(2):
        @pl.when(ends[side])
        def _():
            for cp in row_copies(side):
                cp.start()
    straight = [copy(pack.at[p], colbuf.at[p, pl.ds(0, fold), :], col_send.at[p, 0], col_recv.at[p, 0], to_a, r)
                for p, to_a in ((0, al), (1, ar))]
    for cp in straight:
        cp.start()

    for side in range(2):
        @pl.when(ends[1 - side])
        def _():
            for cp in row_copies_in(side, rowbuf, colbuf, copy, row_send, row_recv, col_send, col_recv, gs, rs, pack, h, a, r):
                cp.wait_recv()
    for cp in straight:
        cp.wait_recv()
    at = (h, 8 * s0 - HALO)
    for k in range(2):
        for gj in range(8):
            for t in range(tiles + 1):
                stage[k, gj, t, pl.ds(h + HALO, 8 * s0 - h - 2 * HALO), :] = jnp.zeros((8 * s0 - h - 2 * HALO, 128), F32)
    def put_edges(gj, t, value):
        for k in range(2):
            for side in range(2):
                n = 2 * k + side
                stage[k, gj, t, pl.ds(at[side], HALO), :] = value[n * HALO:(n + 1) * HALO]

    split_rows(lambda cols: jnp.concatenate(
        [jnp.where(ends[1 - side], rowbuf[k, side, :, cols], 0.0) for k in range(2) for side in range(2)], axis=0),
        4 * HALO, put_edges)

    def beside(first, count, shift):
        right, left = colbuf[0, pl.ds(first, count), :], colbuf[1, pl.ds(first, count), :]
        return jnp.where(lane((count, 128)) < 32, roll(right, -shift, 1), roll(left, 32 - shift, 1))

    strips = [beside(0, fold, 32 * q) for q in range(4)]
    strips.append(jnp.where(ends[1], beside(fold, HALO, 0), 0.0))
    strips.append(jnp.where(ends[0], beside(fold + HALO, HALO, 96), 0.0))
    strips = jnp.concatenate(strips, axis=0)
    for k in range(2):
        y = permute(strips, halo_spread[k])
        for gj in range(8):
            cols = slice(gj * 128, gj * 128 + 128)
            stage[k, gj, tiles, pl.ds(0, h + HALO), :] = y[0:h + HALO, cols]
            stage[k, gj, tiles, pl.ds(at[1], HALO), :] = y[h + HALO:, cols]
    for k, dst in enumerate((v0, g0)):
        for gj in range(8):
            for gi in range(8):
                for t in range(tiles + 1):
                    dst[gi, gj, :, t * 128:t * 128 + 128] = stage[k, gj, t, pl.ds(gi, s0, stride=8), :]

    fine = Grid(v0, g0, c0, 8, 8, False)
    middle = Grid(v1, g1, c1, 4, 4, False)
    coarse = Grid(v2, g2, c2, 2, 2, False)
    window = Grid(v3, None, None, 1, 1, False)

    def into(ref):
        def put(gi, gj, value):
            ref[gi, gj] = value
        return put

    fine.sweeps(PRE, False)

    def put1(gi, gj, value):
        g1[gi, gj, 0:blk, 0:lanes] = value[0:blk, 0:lanes]
    fine.restrict(tmp_res, tmp_mid, put1)

    for side, first in ((0, blk), (1, blk + 8)):
        @pl.when(jnp.logical_not(ends[1 - side]))
        def _():
            g1[:, :, first:first + 8, 0:lanes] = jnp.zeros((4, 4, 8, lanes), F32)
    slot = lane((blk, 128)) // 8
    left_edge = right_edge = None
    for g in range(16):
        lo = roll(g1[g // 4, g % 4, 0:blk, 0:128], 8 * g, 1)
        hi = roll(g1[g // 4, g % 4, 0:blk, lanes - 128:lanes], 8 * g + 8, 1)
        left_edge = lo if g == 0 else jnp.where(slot == g, lo, left_edge)
        right_edge = hi if g == 0 else jnp.where(slot == g, hi, right_edge)
    s1[0] = left_edge
    s1[1] = right_edge

    def copies1(side, to_r):
        first = 0 if side == 0 else blk - 8
        made = [copy(g1.at[:, :, pl.ds(first, 8), pl.ds(0, lanes)], g1.at[:, :, pl.ds(blk + 8 * side, 8), pl.ds(0, lanes)],
                     row1_send.at[side], row1_recv.at[side], a, to_r)]
        for p, to_a in ((0, al), (1, ar)):
            made.append(copy(s1.at[p, pl.ds(first, 8), :], q1.at[p, pl.ds(blk + 8 * side, 8), :],
                             col1_send.at[p, 1 + side], col1_recv.at[p, 1 + side], to_a, to_r))
        return made

    straight1 = [copy(s1.at[p], q1.at[p, pl.ds(0, blk), :], col1_send.at[p, 0], col1_recv.at[p, 0], to_a, r)
                 for p, to_a in ((0, al), (1, ar))]
    for side in range(2):
        @pl.when(ends[side])
        def _():
            for cp in copies1(side, r - 1 if side == 0 else r + 1):
                cp.start()
    for cp in straight1:
        cp.start()
    for side in range(2):
        @pl.when(ends[1 - side])
        def _():
            for cp in copies1(side, r + 1 if side == 0 else r - 1):
                cp.wait_recv()
    for cp in straight1:
        cp.wait_recv()
    wl = lane((blk + 16, 128))
    sub = lax.broadcasted_iota(jnp.int32, (blk + 16, 128), 0)
    got = jnp.where(sub < blk, 1, jnp.where(sub < blk + 8, nrad - 1 - r, r)) > 0
    strip_r, strip_l = jnp.where(got, q1[0], 0.0), jnp.where(got, q1[1], 0.0)
    for g in range(16):
        g1[g // 4, g % 4, :, lanes:ext] = jnp.where(
            wl < 8, roll(strip_r, -8 * g, 1), jnp.where(wl >= 120, roll(strip_l, 120 - 8 * g, 1), 0.0))
    middle.sweeps(PRE, True)
    middle.restrict(t1, u1, into(g2))
    coarse.sweeps(PRE, True)

    def put3(gi, gj, value):
        wv[...] = value[0:blk, 0:lanes]
    coarse.restrict(t1, u1, put3)

    place = gat.at[a, pl.ds(pl.multiple_of(r * blk, 8), blk), :]
    gat[a, pl.ds(pl.multiple_of(r * blk, 8), blk), :] = wv[...]

    def hand(da, dr):
        step = da * nrad + dr
        return copy(wv, place, all_send.at[step], all_recv.at[step], lax.rem(a + da, na), lax.rem(r + dr, nrad))

    for d in others:
        hand(*d).start()
    for d in others:
        hand(*d).wait_recv()

    w3 = lanes * na
    q3 = w3 // 4
    for aa in range(na):
        for t in range(tiles):
            rows3[aa * tiles + t] = gat[aa, :, t * 128:t * 128 + 128]
    stacked = jnp.concatenate([jnp.concatenate(
        [rows3[t, pl.ds(gi, nrad, stride=16), :] for t in range(na * tiles)], axis=1) for gi in range(16)], axis=0)
    table3 = one_hot(w3, w3, lambda c: 4 * (c % q3) + c // q3)
    by_group = permute(stacked, table3)
    for gi in range(16):
        for gj in range(4):
            b3[gi, gj] = by_group[gi * nrad:(gi + 1) * nrad, gj * q3:(gj + 1) * q3]

    l3 = Grid(a3, b3, d3, 16, 4, True)
    l4 = Grid(a4, b4, d4, 8, 2, True)
    l5 = Grid(a5, b5, d5, 4, 4, True)
    l6 = Grid(a6, b6, d6, 2, 2, True)
    l3.sweeps(PRE, True)
    l3.restrict(t3, u3, into(b4))
    l4.sweeps(PRE, True)
    w5 = w3 // 4
    q5 = w5 // 4
    nat5 = {}

    def put5(gi, gj, value):
        nat5[gi] = value
    l4.restrict(t3, u3, put5)
    x5 = permute(jnp.concatenate([nat5[i] for i in range(4)], axis=0),
                 one_hot(w5, 512, lambda c: 4 * (c % q5) + c // 128))
    for gi in range(4):
        for gj in range(4):
            b5[gi, gj] = x5[gi * nrad:(gi + 1) * nrad, gj * 128:gj * 128 + 128]
    l5.sweeps(PRE, True)
    l5.restrict(tmp_small(t3), tmp_small(u3), into(b6))
    l6.sweeps(PRE, True)
    l6.restrict(tmp_small(t3), tmp_small(u3), into(b7))
    l7 = Grid(a7, b7, d7, 1, 1, True)
    red = (lax.broadcasted_iota(jnp.int32, (nrad, 128), 0) + lane((nrad, 128))) % 2 == 0
    a7[0, 0] = jnp.zeros((nrad, 128), F32)

    def coarsest(_, carry):
        a7[0, 0] = jnp.where(red, l7.update(0, 0), a7[0, 0])
        a7[0, 0] = jnp.where(red, a7[0, 0], l7.update(0, 0))
        return carry
    lax.fori_loop(0, COARSE_SWEEPS, coarsest, 0)

    l6.add_prolonged(l7, tmp_small(t3), False)
    l6.sweeps(POST, False)
    l5.add_prolonged(l6, tmp_small(t3), False)
    l5.sweeps(POST, False)
    y5 = None
    for gj in range(4):
        x = jnp.concatenate([a5[gi, gj] for gi in range(4)], axis=0)
        r0 = permute(x, one_hot(128, w5, lambda c, gj=gj: jnp.where(c % 4 == gj, c // 4, -1)))
        y5 = r0 if y5 is None else y5 + r0
    for gi in range(4):
        u3[gi, 0] = y5[gi * nrad:(gi + 1) * nrad]
    l4.add_prolonged(Grid(u3, None, None, 4, 1, True), t3, False)
    l4.sweeps(POST, False)
    l3.add_prolonged(l4, t3, False)
    l3.sweeps(POST, False)

    for gj in range(4):
        for t in range(q3 // 128):
            nat3[gj * (q3 // 128) + t, pl.ds(0, 8), :] = jnp.zeros((8, 128), F32)
            nat3[gj * (q3 // 128) + t, pl.ds(8 + 16 * nrad, 8), :] = jnp.zeros((8, 128), F32)
            for gi in range(16):
                nat3[gj * (q3 // 128) + t, pl.ds(8 + gi, nrad, stride=16), :] = a3[gi, gj, :, t * 128:t * 128 + 128]
    begin = pl.multiple_of(r * 16, 8)
    x3 = jnp.concatenate([nat3[t, pl.ds(begin, 32), :] for t in range(w3 // 128)], axis=1)
    x3 = jnp.concatenate([x3[8:24], x3[24:32], x3[0:8]], axis=0)
    y3 = permute(x3, one_hot(w3, w3, lambda c: (c % 4) * q3 + c // 4))
    for aa in range(na):
        wg[aa] = y3[:, aa * lanes:(aa + 1) * lanes]
    v3[0, 0, :, 0:lanes] = wg[a]
    v3[0, 0, :, lanes:ext] = jnp.where(lane((32, 128)) < 64, wg[ar, :, 0:128], wg[al, :, lanes - 128:lanes])

    coarse.add_prolonged(window, t1, True)
    coarse.sweeps(POST, False)
    middle.add_prolonged(coarse, t1, True)
    middle.sweeps(POST, False)
    near_end = lax.broadcasted_iota(jnp.int32, (8, ext), 0) < 4
    fine.add_prolonged(middle, tmp_res, True, lambda x: jnp.concatenate(
        [x[0:blk], jnp.where(near_end, x[blk:blk + 8], x[blk + 8:blk + 16])], axis=0))
    fine.sweeps(POST, False)

    for gi in range(8):
        centre = fine.coef(4, gi)
        out_c, in_c, ang_c = (fine.coef(k, gi) * centre for k in (1, 2, 3))
        for gj in range(8):
            full = (g0[gi, gj] + out_c * fine.up(v0, gi, gj) + in_c * fine.down(v0, gi, gj)
                    + ang_c * (fine.right(v0, gi, gj) + fine.left(v0, gi, gj)) - centre * v0[gi, gj])
            for t in range(tiles):
                cols = slice(t * 128, t * 128 + 128)
                sol[gj, t, pl.ds(gi, blk, stride=8), :] = v0[gi, gj, 0:blk, cols]
                resid[gj, t, pl.ds(gi, blk, stride=8), :] = full[0:blk, cols]
    for side in range(2):
        @pl.when(ends[side])
        def _():
            for cp in row_copies(side):
                cp.wait_send()
    for cp in straight:
        cp.wait_send()
    for side in range(2):
        @pl.when(ends[side])
        def _():
            for cp in copies1(side, r - 1 if side == 0 else r + 1):
                cp.wait_send()
    for cp in straight1:
        cp.wait_send()
    for d in others:
        hand(*d).wait_send()


def join_kernel(grouped_sol, grouped_res, sol, resid):
    tiles, h = grouped_sol.shape[1:3]
    join = one_hot(256, 256, lambda c: 32 * (c % 8) + c // 8)
    ln = lax.broadcasted_iota(jnp.int32, (h, 128), 1) // 32
    for x, out in ((grouped_sol, sol), (grouped_res, resid)):
        for t in range(tiles):
            for b in range(4):
                halves = []
                for hf in range(2):
                    o = None
                    for p in range(4):
                        piece = roll(x[hf * 4 + p, t], 32 * (p - b), 1)
                        o = piece if o is None else jnp.where(ln == p, piece, o)
                    halves.append(o)
                base = (4 * t + b) * 256
                out[:, base:base + 256] = permute(jnp.concatenate(halves, axis=1), join)


def row_copies_in(side, rowbuf, colbuf, copy, row_send, row_recv, col_send, col_recv, gs, rs, pack, h, a, r):
    rows = pl.ds(0, HALO)
    to_r = r + 1 if side == 0 else r - 1
    made = [copy(x.at[rows, :], rowbuf.at[k, side], row_send.at[k, side], row_recv.at[k, side], a, to_r)
            for k, x in enumerate((gs, rs))]
    for p in range(2):
        made.append(copy(pack.at[p, rows, :], colbuf.at[p, pl.ds(h // 4 + side * HALO, HALO), :],
                         col_send.at[p, 1 + side], col_recv.at[p, 1 + side], a, to_r))
    return made


def tmp_small(ref):
    return ref.at[:, :, :, 0:128]


def solution(mesh):
    na, nrad = mesh.shape["ang"], mesh.shape["rad"]

    def local(right_side, guess):
        h, w = right_side.shape
        lanes = w // 8
        ext, tiles = lanes + 128, lanes // 128
        blk = h // 8
        s0 = blk + 8
        w3, q3 = lanes * na, lanes * na // 4
        m = lambda *s: pltpu.VMEM(s, F32)
        scratch = [
            m(h, w), m(h, w), pltpu.SemaphoreType.DMA((2,)),
            m(2, 2, HALO, w), m(2, h // 4, 128), m(2, h // 4 + 2 * HALO, 128), m(2, blk, 128), m(2, blk + 16, 128), m(4, 4, 32, ext), m(4, 4, 32, ext),
            m(2, 8, tiles + 1, 8 * s0, 128),
            m(8, 8, s0, ext), m(8, 8, s0, ext), m(6, 8, s0, 128),
            m(4, 4, 32, ext), m(4, 4, 32, ext), m(6, 4, 32, 128),
            m(2, 2, 32, ext), m(2, 2, 32, ext), m(6, 2, 32, 128),
            m(1, 1, 32, ext), m(6, 1, 32, 128),
            m(h // 8, lanes), m(na, 32, lanes), m(8, 8, s0, ext), m(4, 8, s0, ext),
            m(na, nrad * 16, lanes), m(na * tiles, nrad * 16, 128), m(w3 // 128, nrad * 16 + 16, 128),
            m(16, 4, nrad, q3), m(16, 4, nrad, q3), m(6, 16, nrad, 128),
            m(8, 2, nrad, q3), m(8, 2, nrad, q3), m(6, 8, nrad, 128),
            m(4, 4, nrad, 128), m(4, 4, nrad, 128), m(6, 4, nrad, 128),
            m(2, 2, nrad, 128), m(2, 2, nrad, 128), m(6, 2, nrad, 128),
            m(1, 1, nrad, 128), m(1, 1, nrad, 128), m(6, 1, nrad, 128),
            m(16, 4, nrad, q3), m(8, 4, nrad, q3),
            pltpu.SemaphoreType.DMA((2, 2)), pltpu.SemaphoreType.DMA((2, 2)),
            pltpu.SemaphoreType.DMA((2, 3)), pltpu.SemaphoreType.DMA((2, 3)),
            pltpu.SemaphoreType.DMA((2,)), pltpu.SemaphoreType.DMA((2,)),
            pltpu.SemaphoreType.DMA((2, 3)), pltpu.SemaphoreType.DMA((2, 3)),
            pltpu.SemaphoreType.DMA((na * nrad,)), pltpu.SemaphoreType.DMA((na * nrad,)),
        ]
        grouped = pl.pallas_call(
            lambda *refs: kernel(na, nrad, h, w, *refs),
            out_shape=[jax.ShapeDtypeStruct((8, tiles, h, 128), F32)] * 2,
            in_specs=[pl.BlockSpec(memory_space=pl.ANY)] * 2,
            out_specs=[pl.BlockSpec(memory_space=pltpu.VMEM)] * 2,
            scratch_shapes=scratch,
            compiler_params=pltpu.CompilerParams(has_side_effects=True, collective_id=0, vmem_limit_bytes=60 * 1024 * 1024),
        )(right_side, guess)
        part = h // 2
        return pl.pallas_call(
            join_kernel,
            out_shape=[jax.ShapeDtypeStruct((h, w), F32)] * 2,
            grid=(2,),
            in_specs=[pl.BlockSpec((8, tiles, part, 128), lambda i: (0, 0, i, 0))] * 2,
            out_specs=[pl.BlockSpec((part, w), lambda i: (i, 0))] * 2,
        )(*grouped)

    placed = (P("rad", "ang"), P("rad", "ang"))
    return jax.shard_map(local, mesh=mesh, in_specs=placed, out_specs=placed, check_vma=False)
```

profile of v0, /device:TPU:0, one launch (start us, length us, event | category | flops | bytes accessed | tf_op | source)
XLA Modules:
  0.0 38.7 jit_solution(9765929713530839540)
XLA Ops:
  0.6 35.0 %shard_map.41 = (f32[8,1,128,128]{3,2,1,0:T(8,128)}, f32[8,1,128,128]{3,2,1,0:T(8,128)}) custom-call(f32[128,1024]{1,0:T(8,128)} %refs_0_.1, f32[128,1024]{1,0:T(8,128)} %refs_1_.1), custom_call_target="tpu_custom_call" | custom-call | tf_op jit(solution)/shard_map/pallas_call | solution.py:549
  35.6 3.1 %shard_map.42 = (f32[128,1024]{1,0:T(8,128)}, f32[128,1024]{1,0:T(8,128)}) custom-call(f32[8,1,128,128]{3,2,1,0:T(8,128)} %get-tuple-element.4.grouped_sol, f32[8,1,128,128]{3,2,1,0:T(8,128)} %get-tuple-element.5.grouped_res), custom_call_target="tpu_custom_call" | custom-call | tf_op jit(solution)/shard_map/pallas_call | solution.py:558
where the time goes:
time: 38.9 us; the launch traced here: 38.7 us
  Pallas kernels  38.1 us (98%)
  between operations  0.64 us (2%)
    pallas_call x1, Pallas kernels, local(): pl.pallas_call(lambda *refs: kernel(na, nrad, h, w, *refs), out_shape=[ja...  35 us
    pallas_call x1, Pallas kernels, local(): pl.pallas_call(join_kernel, out_shape=[jax.ShapeDtypeStruct((h, w), F32)]...  3.13 us

commit v1 on v0

--- a/solution.py
+++ b/solution.py
@@ -173,6 +173,11 @@
     for da, dr in others:
         pl.semaphore_signal(barrier, inc=1, device_id=(lax.rem(a + da, na), lax.rem(r + dr, nrad)), device_id_type=MESH)
 
+    for l, c in ((0, c0), (1, c1), (2, c2)):
+        fill_coefficients(c, 8 >> l, s0 if l == 0 else blk + 16, r * (h >> l), (h * nrad) >> l, spacing[l], blk + 4 if l == 0 else blk + 8)
+    for l, d, n in ((3, d3, 16), (4, d4, 8), (5, d5, 4), (6, d6, 2), (7, d7, 1)):
+        fill_coefficients(d, n, nrad, 0, (h * nrad) >> l, spacing[l], 0)
+
     for cp in loads:
         cp.wait()
 
@@ -200,10 +205,17 @@
                              col_send.at[p, 1 + side], col_recv.at[p, 1 + side], to_a, to_r))
         return made
 
-    for l, c in ((0, c0), (1, c1), (2, c2)):
-        fill_coefficients(c, 8 >> l, s0 if l == 0 else blk + 16, r * (h >> l), (h * nrad) >> l, spacing[l], blk + 4 if l == 0 else blk + 8)
-    for l, d, n in ((3, d3, 16), (4, d4, 8), (5, d5, 4), (6, d6, 2), (7, d7, 1)):
-        fill_coefficients(d, n, nrad, 0, (h * nrad) >> l, spacing[l], 0)
+    pl.semaphore_wait(barrier, total - 1)
+    ends = (r > 0, r < nrad - 1)
+    for side in range(2):
+        @pl.when(ends[side])
+        def _():
+            for cp in row_copies(side):
+                cp.start()
+    straight = [copy(pack.at[p], colbuf.at[p, pl.ds(0, fold), :], col_send.at[p, 0], col_recv.at[p, 0], to_a, r)
+                for p, to_a in ((0, al), (1, ar))]
+    for cp in straight:
+        cp.start()
 
     spread = one_hot(256, 256, lambda c: 8 * (c % 32) + c // 32)
     halo_spread = [one_hot(128, 1024, lambda c, k=k: jnp.where(
@@ -229,18 +241,6 @@
 
     for k, x in enumerate((gs, rs)):
         split_rows(lambda cols, x=x: x[:, cols], h, put_own(k))
-
-    pl.semaphore_wait(barrier, total - 1)
-    ends = (r > 0, r < nrad - 1)
-    for side in range(2):
-        @pl.when(ends[side])
-        def _():
-            for cp in row_copies(side):
-                cp.start()
-    straight = [copy(pack.at[p], colbuf.at[p, pl.ds(0, fold), :], col_send.at[p, 0], col_recv.at[p, 0], to_a, r)
-                for p, to_a in ((0, al), (1, ar))]
-    for cp in straight:
-        cp.start()
 
     for side in range(2):
         @pl.when(ends[1 - side])

time: 38.9 us -> 38.9 us (level)
  no operation moved by 1% of the time
where the time goes in v1:
time: 38.9 us; the launch traced here: 38.7 us
  Pallas kernels  38.1 us (98%)
  between operations  0.64 us (2%)
    pallas_call x1, Pallas kernels, local(): pl.pallas_call(lambda *refs: kernel(na, nrad, h, w, *refs), out_shape=[ja...  35 us
    pallas_call x1, Pallas kernels, local(): pl.pallas_call(join_kernel, out_shape=[jax.ShapeDtypeStruct((h, w), F32)]...  3.13 us

profile of v1, /device:TPU:0, one launch (start us, length us, event | category | flops | bytes accessed | tf_op | source)
XLA Modules:
  0.0 38.7 jit_solution(18116066095992887949)
XLA Ops:
  0.6 35.0 %shard_map.41 = (f32[8,1,128,128]{3,2,1,0:T(8,128)}, f32[8,1,128,128]{3,2,1,0:T(8,128)}) custom-call(f32[128,1024]{1,0:T(8,128)} %refs_0_.1, f32[128,1024]{1,0:T(8,128)} %refs_1_.1), custom_call_target="tpu_custom_call" | custom-call | tf_op jit(solution)/shard_map/pallas_call | solution.py:549
  35.6 3.1 %shard_map.42 = (f32[128,1024]{1,0:T(8,128)}, f32[128,1024]{1,0:T(8,128)}) custom-call(f32[8,1,128,128]{3,2,1,0:T(8,128)} %get-tuple-element.4.grouped_sol, f32[8,1,128,128]{3,2,1,0:T(8,128)} %get-tuple-element.5.grouped_res), custom_call_target="tpu_custom_call" | custom-call | tf_op jit(solution)/shard_map/pallas_call | solution.py:558

commit v2 on v1

--- a/solution.py
+++ b/solution.py
@@ -151,7 +151,7 @@
 def kernel(na, nrad, h, w, rs_in, gs_in, sol, resid, rs, gs, load_sem,
            rowbuf, pack, colbuf, s1, q1, t1, u1, stage, v0, g0, c0, v1, g1, c1, v2, g2, c2, v3, c3, wv, wg, tmp_res, tmp_mid,
            gat, rows3, nat3, a3, b3, d3, a4, b4, d4, a5, b5, d5, a6, b6, d6, a7, b7, d7, t3, u3,
-           row_send, row_recv, col_send, col_recv, row1_send, row1_recv, col1_send, col1_recv, all_send, all_recv):
+           row_send, row_recv, col_send, col_recv, row1_send, row1_recv, col1_send, col1_recv, all_send, all_recv, known):
     a, r = lax.axis_index("ang"), lax.axis_index("rad")
     ar, al = lax.rem(a + 1, na), lax.rem(a + na - 1, na)
     lanes = w // 8
@@ -165,13 +165,35 @@
         cp.start()
     blk = h // 8
     s0 = blk + 8
-    total = na * nrad
     barrier = pltpu.get_barrier_semaphore()
 
     others = sorted(((da, dr) for da in range(na) for dr in range(nrad) if da or dr),
                     key=lambda d: -min(d[1], nrad - d[1]))
-    for da, dr in others:
-        pl.semaphore_signal(barrier, inc=1, device_id=(lax.rem(a + da, na), lax.rem(r + dr, nrad)), device_id_type=MESH)
+    ends = (r > 0, r < nrad - 1)
+
+    def greet(to_r, first):
+        for da in range(first, na):
+            pl.semaphore_signal(barrier, inc=1, device_id=(lax.rem(a + da, na), to_r), device_id_type=MESH)
+
+    for side in range(2):
+        @pl.when(ends[side])
+        def _():
+            greet(r - 1 if side == 0 else r + 1, 0)
+    greet(r, 1)
+    reach = [2 << k for k in range(nrad.bit_length()) if 2 << k < nrad - 1]
+
+    def announce(k):
+        for side, there in ((0, r >= reach[k]), (1, r < nrad - reach[k])):
+            @pl.when(there)
+            def _():
+                to_r = r - reach[k] if side == 0 else r + reach[k]
+                pl.semaphore_signal(known.at[k, 1 - side], inc=1, device_id=(a, to_r), device_id_type=MESH)
+
+    def learn(k):
+        for side, there in ((0, r >= reach[k]), (1, r < nrad - reach[k])):
+            @pl.when(there)
+            def _():
+                pl.semaphore_wait(known.at[k, side], 1)
 
     for l, c in ((0, c0), (1, c1), (2, c2)):
         fill_coefficients(c, 8 >> l, s0 if l == 0 else blk + 16, r * (h >> l), (h * nrad) >> l, spacing[l], blk + 4 if l == 0 else blk + 8)
@@ -205,8 +227,7 @@
                              col_send.at[p, 1 + side], col_recv.at[p, 1 + side], to_a, to_r))
         return made
 
-    pl.semaphore_wait(barrier, total - 1)
-    ends = (r > 0, r < nrad - 1)
+    pl.semaphore_wait(barrier, na * (1 + (r > 0).astype(jnp.int32) + (r < nrad - 1).astype(jnp.int32)) - 1)
     for side in range(2):
         @pl.when(ends[side])
         def _():
@@ -249,6 +270,7 @@
                 cp.wait_recv()
     for cp in straight:
         cp.wait_recv()
+    announce(0)
     at = (h, 8 * s0 - HALO)
     for k in range(2):
         for gj in range(8):
@@ -332,6 +354,11 @@
                 cp.start()
     for cp in straight1:
         cp.start()
+    learn(0)
+    for k in range(1, len(reach)):
+        announce(k)
+        if k < len(reach) - 1:
+            learn(k)
     for side in range(2):
         @pl.when(ends[1 - side])
         def _():
@@ -361,6 +388,7 @@
         step = da * nrad + dr
         return copy(wv, place, all_send.at[step], all_recv.at[step], lax.rem(a + da, na), lax.rem(r + dr, nrad))
 
+    learn(len(reach) - 1)
     for d in others:
         hand(*d).start()
     for d in others:
@@ -480,11 +508,12 @@
         hand(*d).wait_send()
 
 
-def join_kernel(grouped_sol, grouped_res, sol, resid):
+def join_kernel(grouped_sol, grouped_res, sol, resid, whole, out_sem):
     tiles, h = grouped_sol.shape[1:3]
     join = one_hot(256, 256, lambda c: 32 * (c % 8) + c // 8)
     ln = lax.broadcasted_iota(jnp.int32, (h, 128), 1) // 32
-    for x, out in ((grouped_sol, sol), (grouped_res, resid)):
+    copies = []
+    for k, (x, out) in enumerate(((grouped_sol, sol), (grouped_res, resid))):
         for t in range(tiles):
             for b in range(4):
                 halves = []
@@ -494,8 +523,12 @@
                         piece = roll(x[hf * 4 + p, t], 32 * (p - b), 1)
                         o = piece if o is None else jnp.where(ln == p, piece, o)
                     halves.append(o)
-                base = (4 * t + b) * 256
-                out[:, base:base + 256] = permute(jnp.concatenate(halves, axis=1), join)
+                cols = pl.ds((4 * t + b) * 256, 256)
+                whole[k, :, cols] = permute(jnp.concatenate(halves, axis=1), join)
+                copies.append(pltpu.make_async_copy(whole.at[k, :, cols], out.at[:, cols], out_sem.at[k, 4 * t + b]))
+                copies[-1].start()
+    for cp in copies:
+        cp.wait()
 
 
 def row_copies_in(side, rowbuf, colbuf, copy, row_send, row_recv, col_send, col_recv, gs, rs, pack, h, a, r):
@@ -545,6 +578,7 @@
             pltpu.SemaphoreType.DMA((2,)), pltpu.SemaphoreType.DMA((2,)),
             pltpu.SemaphoreType.DMA((2, 3)), pltpu.SemaphoreType.DMA((2, 3)),
             pltpu.SemaphoreType.DMA((na * nrad,)), pltpu.SemaphoreType.DMA((na * nrad,)),
+            pltpu.SemaphoreType.REGULAR((nrad.bit_length(), 2)),
         ]
         grouped = pl.pallas_call(
             lambda *refs: kernel(na, nrad, h, w, *refs),
@@ -552,15 +586,15 @@
             in_specs=[pl.BlockSpec(memory_space=pl.ANY)] * 2,
             out_specs=[pl.BlockSpec(memory_space=pltpu.VMEM)] * 2,
             scratch_shapes=scratch,
-            compiler_params=pltpu.CompilerParams(has_side_effects=True, collective_id=0, vmem_limit_bytes=60 * 1024 * 1024),
+            compiler_params=pltpu.CompilerParams(has_side_effects=True, collective_id=0, vmem_limit_bytes=105 * 512 * 1024),
         )(right_side, guess)
-        part = h // 2
         return pl.pallas_call(
             join_kernel,
             out_shape=[jax.ShapeDtypeStruct((h, w), F32)] * 2,
-            grid=(2,),
-            in_specs=[pl.BlockSpec((8, tiles, part, 128), lambda i: (0, 0, i, 0))] * 2,
-            out_specs=[pl.BlockSpec((part, w), lambda i: (i, 0))] * 2,
+            in_specs=[pl.BlockSpec(memory_space=pltpu.VMEM)] * 2,
+            out_specs=[pl.BlockSpec(memory_space=pl.ANY)] * 2,
+            scratch_shapes=[m(2, h, w), pltpu.SemaphoreType.DMA((2, 4 * tiles))],
+            compiler_params=pltpu.CompilerParams(vmem_limit_bytes=16 * 1024 * 1024),
         )(*grouped)
 
     placed = (P("rad", "ang"), P("rad", "ang"))

time: 38.9 us -> 36.9 us (0.949)
  Pallas kernels: 38.1 us -> 36.1 us
    pallas_call x1, Pallas kernels: 3.13 us -> 1.87 us  [local(): pl.pallas_call(join_kernel, out_shape=[jax.ShapeDtypeStruct((h, w), F32)]...]
    pallas_call x1, Pallas kernels: 35 us -> 34.2 us  [local(): pl.pallas_call(lambda *refs: kernel(na, nrad, h, w, *refs), out_shape=[ja...]
where the time goes in v2:
time: 36.9 us; the launch traced here: 36.7 us
  Pallas kernels  36.1 us (98%)
  between operations  0.64 us (2%)
    pallas_call x1, Pallas kernels, local(): pl.pallas_call(lambda *refs: kernel(na, nrad, h, w, *refs), out_shape=[ja...  34.2 us
    pallas_call x1, Pallas kernels, local(): pl.pallas_call(join_kernel, out_shape=[jax.ShapeDtypeStruct((h, w), F32)]...  1.87 us

profile of v2, /device:TPU:0, one launch (start us, length us, event | category | flops | bytes accessed | tf_op | source)
XLA Modules:
  0.0 36.7 jit_solution(4279198977266929201)
XLA Ops:
  0.6 34.2 %shard_map.41 = (f32[8,1,128,128]{3,2,1,0:T(8,128)S(1)}, f32[8,1,128,128]{3,2,1,0:T(8,128)S(1)}) custom-call(f32[128,1024]{1,0:T(8,128)} %refs_0_.1, f32[128,1024]{1,0:T(8,128)} %refs_1_.1), custom_call_target="tpu_custom_call" | custom-call | tf_op jit(solution)/shard_map/pallas_call | solution.py:583
  34.9 1.9 %shard_map.42 = (f32[128,1024]{1,0:T(8,128)}, f32[128,1024]{1,0:T(8,128)}) custom-call(f32[8,1,128,128]{3,2,1,0:T(8,128)S(1)} %get-tuple-element.4.grouped_sol, f32[8,1,128,128]{3,2,1,0:T(8,128)S(1)} %get-tuple-element.5.grouped_res), custom_call_target="tpu_custom_call" | custom-call | tf_op jit(solution)/shard_map/pallas_call | solution.py:591

commit v3 on v2

--- a/solution.py
+++ b/solution.py
@@ -167,7 +167,7 @@
     s0 = blk + 8
     barrier = pltpu.get_barrier_semaphore()
 
-    others = sorted(((da, dr) for da in range(na) for dr in range(nrad) if da or dr),
+    others = sorted(((da, dr) for da in range(na) for dr in range(0, nrad, 2) if da or dr),
                     key=lambda d: -min(d[1], nrad - d[1]))
     ends = (r > 0, r < nrad - 1)
 
@@ -231,12 +231,17 @@
     for side in range(2):
         @pl.when(ends[side])
         def _():
-            for cp in row_copies(side):
+            for cp in row_copies(side)[2:]:
                 cp.start()
     straight = [copy(pack.at[p], colbuf.at[p, pl.ds(0, fold), :], col_send.at[p, 0], col_recv.at[p, 0], to_a, r)
                 for p, to_a in ((0, al), (1, ar))]
     for cp in straight:
         cp.start()
+    for side in range(2):
+        @pl.when(ends[side])
+        def _():
+            for cp in row_copies(side)[:2]:
+                cp.start()
 
     spread = one_hot(256, 256, lambda c: 8 * (c % 32) + c // 32)
     halo_spread = [one_hot(128, 1024, lambda c, k=k: jnp.where(
@@ -350,10 +355,14 @@
     for side in range(2):
         @pl.when(ends[side])
         def _():
-            for cp in copies1(side, r - 1 if side == 0 else r + 1):
+            for cp in copies1(side, r - 1 if side == 0 else r + 1)[1:]:
                 cp.start()
     for cp in straight1:
         cp.start()
+    for side in range(2):
+        @pl.when(ends[side])
+        def _():
+            copies1(side, r - 1 if side == 0 else r + 1)[0].start()
     learn(0)
     for k in range(1, len(reach)):
         announce(k)
@@ -388,11 +397,24 @@
         step = da * nrad + dr
         return copy(wv, place, all_send.at[step], all_recv.at[step], lax.rem(a + da, na), lax.rem(r + dr, nrad))
 
+    partner = r + 1 - 2 * lax.rem(r, 2)
+
+    def relay(da, dr):
+        step = da * nrad + dr + 1
+        came = gat.at[lax.rem(a + na - da, na), pl.ds(pl.multiple_of(lax.rem(r + nrad - dr, nrad) * blk, 8), blk), :]
+        return copy(came, came, all_send.at[step], all_recv.at[step], a, partner)
+
+    own = copy(wv, place, all_send.at[0], all_recv.at[0], a, partner)
     learn(len(reach) - 1)
     for d in others:
         hand(*d).start()
-    for d in others:
+    own.start()
+    for d in reversed(others):
         hand(*d).wait_recv()
+        relay(*d).start()
+    own.wait_recv()
+    for d in reversed(others):
+        relay(*d).wait_recv()
 
     w3 = lanes * na
     q3 = w3 // 4
@@ -504,8 +526,10 @@
                 cp.wait_send()
     for cp in straight1:
         cp.wait_send()
+    own.wait_send()
     for d in others:
         hand(*d).wait_send()
+        relay(*d).wait_send()
 
 
 def join_kernel(grouped_sol, grouped_res, sol, resid, whole, out_sem):

time: 36.9 us -> 34.1 us (0.924)
  the two profiles are of different devices: /device:TPU:0 before, /device:TPU:1 now
where the time goes in v3:
time: 34.1 us; the launch traced here: 34 us
  Pallas kernels  33.3 us (98%)
  between operations  0.64 us (2%)
    pallas_call x1, Pallas kernels, local(): pl.pallas_call(lambda *refs: kernel(na, nrad, h, w, *refs), out_shape=[ja...  31.5 us
    pallas_call x1, Pallas kernels, local(): pl.pallas_call(join_kernel, out_shape=[jax.ShapeDtypeStruct((h, w), F32)]...  1.87 us

profile of v3, /device:TPU:1, one launch (start us, length us, event | category | flops | bytes accessed | tf_op | source)
XLA Modules:
  0.0 34.0 jit_solution(10349480897605454543)
XLA Ops:
  0.6 31.5 %shard_map.41 = (f32[8,1,128,128]{3,2,1,0:T(8,128)S(1)}, f32[8,1,128,128]{3,2,1,0:T(8,128)S(1)}) custom-call(f32[128,1024]{1,0:T(8,128)} %refs_0_.1, f32[128,1024]{1,0:T(8,128)} %refs_1_.1), custom_call_target="tpu_custom_call" | custom-call | tf_op jit(solution)/shard_map/pallas_call | solution.py:607
  32.1 1.9 %shard_map.42 = (f32[128,1024]{1,0:T(8,128)}, f32[128,1024]{1,0:T(8,128)}) custom-call(f32[8,1,128,128]{3,2,1,0:T(8,128)S(1)} %get-tuple-element.4.grouped_sol, f32[8,1,128,128]{3,2,1,0:T(8,128)S(1)} %get-tuple-element.5.grouped_res), custom_call_target="tpu_custom_call" | custom-call | tf_op jit(solution)/shard_map/pallas_call | solution.py:615

commit v4 on v3

--- a/solution.py
+++ b/solution.py
@@ -2,6 +2,7 @@
 
 import jax
 import jax.numpy as jnp
+import numpy as np
 from jax import lax
 from jax.experimental import pallas as pl
 from jax.experimental.pallas import tpu as pltpu
@@ -38,6 +39,47 @@
 
 def roll(x, shift, axis):
     return pltpu.roll(x, shift % x.shape[axis], axis)
+
+
+def coarsest_operator(rows, cols, spacing):
+    radius = (1.0 + (np.arange(rows) + 0.5) * spacing)[:, None]
+    outward, inward, angular = 1.0 + 0.5 * spacing / radius, 1.0 - 0.5 * spacing / radius, 1.0 / (radius * radius)
+    colour = (np.arange(rows)[:, None] + np.arange(cols)[None, :]) % 2
+    g = np.eye(rows * cols).reshape(-1, rows, cols)
+    v = np.zeros_like(g)
+    for step in range(2 * COARSE_SWEEPS):
+        p = np.pad(v, ((0, 0), (1, 1), (0, 0)))
+        new = (g + outward * p[:, 2:] + inward * p[:, :-2] + angular * (np.roll(v, -1, 2) + np.roll(v, 1, 2))) / (2.0 + 2.0 * angular)
+        v = np.where(colour == step % 2, new, v)
+    rest, parts = v.reshape(rows * cols, rows * cols), []
+    for _ in range(3):
+        parts.append(rest.astype(np.float32).astype(jnp.bfloat16))
+        rest = rest - parts[-1].astype(np.float64)
+    return np.concatenate(parts, axis=1)
+
+
+def apply_operator(x, table, cols):
+    rows, per = x.shape[0], 128 // cols
+    tiles = table.shape[0] // 128
+    s = lax.broadcasted_iota(jnp.int32, x.shape, 0)
+    block = lax.broadcasted_iota(jnp.int32, x.shape, 1) // cols
+    flat = jnp.concatenate([jnp.where(s == t * per + block, x, 0.0) for t in range(tiles)], axis=1)
+    flat = jnp.broadcast_to(jnp.sum(flat, axis=0, keepdims=True), (rows, flat.shape[1]))
+    hi = flat.astype(jnp.bfloat16).astype(F32)
+    mid = (flat - hi).astype(jnp.bfloat16).astype(F32)
+    low = flat - hi - mid
+    lhs = [hi, mid, low] + [jnp.zeros_like(low)] * (3 * rows // 8 % 2)
+    y = jnp.dot(jnp.concatenate(lhs, axis=0).astype(jnp.bfloat16), table, preferred_element_type=F32)
+    out = None
+    for t in range(tiles):
+        piece = lambda k, m: y[k * rows:(k + 1) * rows, (m * tiles + t) * 128:(m * tiles + t) * 128 + 128]
+        total = (piece(0, 2) + piece(1, 1) + piece(2, 0)) + (piece(0, 1) + piece(1, 0)) + piece(0, 0)
+        out = total if out is None else jnp.where(s // per == t, total, out)
+    turn = (block + per - s % per) % per
+    spread = out
+    for k in range(1, per):
+        spread = jnp.where(turn == k, roll(out, cols * k, 1), spread)
+    return spread
 
 
 class Grid:
@@ -148,10 +190,10 @@
             c[k, gi] = jnp.where(inside, value, zero)
 
 
-def kernel(na, nrad, h, w, rs_in, gs_in, sol, resid, rs, gs, load_sem,
+def kernel(na, nrad, h, w, rs_in, gs_in, table_in, sol, resid, rs, gs, load_sem,
            rowbuf, pack, colbuf, s1, q1, t1, u1, stage, v0, g0, c0, v1, g1, c1, v2, g2, c2, v3, c3, wv, wg, tmp_res, tmp_mid,
-           gat, rows3, nat3, a3, b3, d3, a4, b4, d4, a5, b5, d5, a6, b6, d6, a7, b7, d7, t3, u3,
-           row_send, row_recv, col_send, col_recv, row1_send, row1_recv, col1_send, col1_recv, all_send, all_recv, known):
+           gat, rows3, nat3, a3, b3, d3, a4, b4, d4, a5, b5, d5, a6, b6, d6, a7, b7, t3, u3,
+           row_send, row_recv, col_send, col_recv, row1_send, row1_recv, col1_send, col1_recv, all_send, all_recv, known, table7, table_sem):
     a, r = lax.axis_index("ang"), lax.axis_index("rad")
     ar, al = lax.rem(a + 1, na), lax.rem(a + na - 1, na)
     lanes = w // 8
@@ -163,6 +205,8 @@
     loads = [pltpu.make_async_copy(src, dst, load_sem.at[k]) for k, (src, dst) in enumerate(((gs_in, gs), (rs_in, rs)))]
     for cp in loads:
         cp.start()
+    load_table = pltpu.make_async_copy(table_in.at[:, 0:table7.shape[1]], table7, table_sem)
+    load_table.start()
     blk = h // 8
     s0 = blk + 8
     barrier = pltpu.get_barrier_semaphore()
@@ -197,7 +241,7 @@
 
     for l, c in ((0, c0), (1, c1), (2, c2)):
         fill_coefficients(c, 8 >> l, s0 if l == 0 else blk + 16, r * (h >> l), (h * nrad) >> l, spacing[l], blk + 4 if l == 0 else blk + 8)
-    for l, d, n in ((3, d3, 16), (4, d4, 8), (5, d5, 4), (6, d6, 2), (7, d7, 1)):
+    for l, d, n in ((3, d3, 16), (4, d4, 8), (5, d5, 4), (6, d6, 2)):
         fill_coefficients(d, n, nrad, 0, (h * nrad) >> l, spacing[l], 0)
 
     for cp in loads:
@@ -409,6 +453,7 @@
     for d in others:
         hand(*d).start()
     own.start()
+    load_table.wait()
     for d in reversed(others):
         hand(*d).wait_recv()
         relay(*d).start()
@@ -452,15 +497,8 @@
     l5.restrict(tmp_small(t3), tmp_small(u3), into(b6))
     l6.sweeps(PRE, True)
     l6.restrict(tmp_small(t3), tmp_small(u3), into(b7))
-    l7 = Grid(a7, b7, d7, 1, 1, True)
-    red = (lax.broadcasted_iota(jnp.int32, (nrad, 128), 0) + lane((nrad, 128))) % 2 == 0
-    a7[0, 0] = jnp.zeros((nrad, 128), F32)
-
-    def coarsest(_, carry):
-        a7[0, 0] = jnp.where(red, l7.update(0, 0), a7[0, 0])
-        a7[0, 0] = jnp.where(red, a7[0, 0], l7.update(0, 0))
-        return carry
-    lax.fori_loop(0, COARSE_SWEEPS, coarsest, 0)
+    a7[0, 0] = apply_operator(b7[0, 0], table7[...], w * na >> 7)
+    l7 = Grid(a7, None, None, 1, 1, True)
 
     l6.add_prolonged(l7, tmp_small(t3), False)
     l6.sweeps(POST, False)
@@ -581,6 +619,10 @@
         s0 = blk + 8
         w3, q3 = lanes * na, lanes * na // 4
         m = lambda *s: pltpu.VMEM(s, F32)
+        last = LEVELS - 1
+        table = coarsest_operator(h * nrad >> last, w * na >> last, 2.0 * math.pi / (w * na >> last))
+        table7 = pltpu.VMEM(table.shape, jnp.bfloat16)
+        table = jnp.asarray(np.pad(table, ((0, 0), (0, max(0, 5 * h * w // table.shape[0] - table.shape[1])))))
         scratch = [
             m(h, w), m(h, w), pltpu.SemaphoreType.DMA((2,)),
             m(2, 2, HALO, w), m(2, h // 4, 128), m(2, h // 4 + 2 * HALO, 128), m(2, blk, 128), m(2, blk + 16, 128), m(4, 4, 32, ext), m(4, 4, 32, ext),
@@ -595,7 +637,7 @@
             m(8, 2, nrad, q3), m(8, 2, nrad, q3), m(6, 8, nrad, 128),
             m(4, 4, nrad, 128), m(4, 4, nrad, 128), m(6, 4, nrad, 128),
             m(2, 2, nrad, 128), m(2, 2, nrad, 128), m(6, 2, nrad, 128),
-            m(1, 1, nrad, 128), m(1, 1, nrad, 128), m(6, 1, nrad, 128),
+            m(1, 1, nrad, 128), m(1, 1, nrad, 128),
             m(16, 4, nrad, q3), m(8, 4, nrad, q3),
             pltpu.SemaphoreType.DMA((2, 2)), pltpu.SemaphoreType.DMA((2, 2)),
             pltpu.SemaphoreType.DMA((2, 3)), pltpu.SemaphoreType.DMA((2, 3)),
@@ -603,15 +645,16 @@
             pltpu.SemaphoreType.DMA((2, 3)), pltpu.SemaphoreType.DMA((2, 3)),
             pltpu.SemaphoreType.DMA((na * nrad,)), pltpu.SemaphoreType.DMA((na * nrad,)),
             pltpu.SemaphoreType.REGULAR((nrad.bit_length(), 2)),
+            table7, pltpu.SemaphoreType.DMA,
         ]
         grouped = pl.pallas_call(
             lambda *refs: kernel(na, nrad, h, w, *refs),
             out_shape=[jax.ShapeDtypeStruct((8, tiles, h, 128), F32)] * 2,
-            in_specs=[pl.BlockSpec(memory_space=pl.ANY)] * 2,
+            in_specs=[pl.BlockSpec(memory_space=pl.ANY)] * 3,
             out_specs=[pl.BlockSpec(memory_space=pltpu.VMEM)] * 2,
             scratch_shapes=scratch,
-            compiler_params=pltpu.CompilerParams(has_side_effects=True, collective_id=0, vmem_limit_bytes=105 * 512 * 1024),
-        )(right_side, guess)
+            compiler_params=pltpu.CompilerParams(has_side_effects=True, collective_id=0, vmem_limit_bytes=53760 * 1024),
+        )(right_side, guess, table)
         return pl.pallas_call(
             join_kernel,
             out_shape=[jax.ShapeDtypeStruct((h, w), F32)] * 2,

time: 34.1 us -> 33.1 us (0.971)
  Pallas kernels: 33.3 us -> 32.3 us
    pallas_call x1, Pallas kernels: 31.5 us -> 30.4 us  [local(): pl.pallas_call(lambda *refs: kernel(na, nrad, h, w, *refs), out_shape=[ja...]
where the time goes in v4:
time: 33.1 us; the launch traced here: 32.9 us
  Pallas kernels  32.3 us (98%)
  between operations  0.64 us (2%)
    pallas_call x1, Pallas kernels, local(): pl.pallas_call(lambda *refs: kernel(na, nrad, h, w, *refs), out_shape=[ja...  30.4 us
    pallas_call x1, Pallas kernels, local(): pl.pallas_call(join_kernel, out_shape=[jax.ShapeDtypeStruct((h, w), F32)]...  1.87 us

profile of v4, /device:TPU:1, one launch (start us, length us, event | category | flops | bytes accessed | tf_op | source)
XLA Modules:
  0.0 32.9 jit_solution(6438869487596442680)
XLA Ops:
  0.6 30.4 %shard_map.50 = (f32[8,1,128,128]{3,2,1,0:T(8,128)S(1)}, f32[8,1,128,128]{3,2,1,0:T(8,128)S(1)}) custom-call(f32[128,1024]{1,0:T(8,128)} %refs_0_.1, f32[128,1024]{1,0:T(8,128)} %refs_1_.1, bf16[256,2560]{1,0:T(8,128)(2,1)} %constant.2.clone.refs_2_), custom_call_target="tpu_custom_call" | custom-call | tf_op jit(solution)/shard_map/pallas_call | solution.py:650
  31.0 1.9 %shard_map.51 = (f32[128,1024]{1,0:T(8,128)}, f32[128,1024]{1,0:T(8,128)}) custom-call(f32[8,1,128,128]{3,2,1,0:T(8,128)S(1)} %get-tuple-element.4.grouped_sol, f32[8,1,128,128]{3,2,1,0:T(8,128)S(1)} %get-tuple-element.5.grouped_res), custom_call_target="tpu_custom_call" | custom-call | tf_op jit(solution)/shard_map/pallas_call | solution.py:658

commit v5 on v4

--- a/solution.py
+++ b/solution.py
@@ -23,14 +23,16 @@
     return jnp.where(r == source(c), 1.0, 0.0).astype(jnp.bfloat16)
 
 
-def permute(x, table):
-    hi = x.astype(jnp.bfloat16)
-    rest = x - hi.astype(F32)
-    mid = rest.astype(jnp.bfloat16)
-    low = (rest - mid.astype(F32)).astype(jnp.bfloat16)
+def permute(x, table, count=3):
+    rest, parts = x, []
+    for k in range(count):
+        parts.append(rest.astype(jnp.bfloat16))
+        if k < count - 1:
+            rest = rest - parts[-1].astype(F32)
     n = x.shape[0]
-    y = jnp.dot(jnp.concatenate([hi, mid, low], axis=0), table, preferred_element_type=F32)
-    return (y[:n] + y[n:2 * n]) + y[2 * n:]
+    y = jnp.dot(jnp.concatenate(parts, axis=0), table, preferred_element_type=F32)
+    total = y[:n] + y[n:2 * n]
+    return total + y[2 * n:] if count == 3 else total
 
 
 def wide(c, lanes):
@@ -82,6 +84,19 @@
     return spread
 
 
+def transpose4(xs):
+    ln = lax.broadcasted_iota(jnp.int32, xs[0].shape, 1) // 32
+
+    def mix(pick):
+        o = pick(0)
+        for q in range(1, 4):
+            o = jnp.where(ln == q, pick(q), o)
+        return o
+
+    turned = [roll(mix(lambda q: xs[(q + s) % 4]), 32 * s, 1) if s else mix(lambda q: xs[q]) for s in range(4)]
+    return [mix(lambda p: turned[(p - b) % 4]) for b in range(4)]
+
+
 class Grid:
     def __init__(self, v, g, c, nr, nc, closed):
         self.v, self.g, self.c, self.nr, self.nc, self.closed = v, g, c, nr, nc, closed
@@ -193,7 +208,7 @@
 def kernel(na, nrad, h, w, rs_in, gs_in, table_in, sol, resid, rs, gs, load_sem,
            rowbuf, pack, colbuf, s1, q1, t1, u1, stage, v0, g0, c0, v1, g1, c1, v2, g2, c2, v3, c3, wv, wg, tmp_res, tmp_mid,
            gat, rows3, nat3, a3, b3, d3, a4, b4, d4, a5, b5, d5, a6, b6, d6, a7, b7, t3, u3,
-           row_send, row_recv, col_send, col_recv, row1_send, row1_recv, col1_send, col1_recv, all_send, all_recv, known, table7, table_sem):
+           row_send, row_recv, col_send, col_recv, row1_send, row1_recv, col1_send, col1_recv, all_send, all_recv, relay_send, known, table7, table_sem):
     a, r = lax.axis_index("ang"), lax.axis_index("rad")
     ar, al = lax.rem(a + 1, na), lax.rem(a + na - 1, na)
     lanes = w // 8
@@ -202,8 +217,10 @@
     spacing = [2.0 * math.pi / (w * na >> l) for l in range(LEVELS)]
     lane = lambda shape: lax.broadcasted_iota(jnp.int32, shape, 1)
 
-    loads = [pltpu.make_async_copy(src, dst, load_sem.at[k]) for k, (src, dst) in enumerate(((gs_in, gs), (rs_in, rs)))]
-    for cp in loads:
+    spans = (pl.ds(0, 128), pl.ds(w - 128, 128), pl.ds(128, w - 256))
+    loads = [[pltpu.make_async_copy(src.at[:, cols], dst.at[:, cols], load_sem.at[k, n])
+              for k, (src, dst) in enumerate(((gs_in, gs), (rs_in, rs)))] for n, cols in enumerate(spans)]
+    for cp in sum(loads, []):
         cp.start()
     load_table = pltpu.make_async_copy(table_in.at[:, 0:table7.shape[1]], table7, table_sem)
     load_table.start()
@@ -211,8 +228,6 @@
     s0 = blk + 8
     barrier = pltpu.get_barrier_semaphore()
 
-    others = sorted(((da, dr) for da in range(na) for dr in range(0, nrad, 2) if da or dr),
-                    key=lambda d: -min(d[1], nrad - d[1]))
     ends = (r > 0, r < nrad - 1)
 
     def greet(to_r, first):
@@ -244,7 +259,7 @@
     for l, d, n in ((3, d3, 16), (4, d4, 8), (5, d5, 4), (6, d6, 2)):
         fill_coefficients(d, n, nrad, 0, (h * nrad) >> l, spacing[l], 0)
 
-    for cp in loads:
+    for cp in loads[0] + loads[1]:
         cp.wait()
 
     fold = h // 4
@@ -263,13 +278,17 @@
 
     def row_copies(side):
         to_r = r - 1 if side == 0 else r + 1
-        rows = pl.ds(0, HALO) if side == 0 else pl.ds(h - HALO, HALO)
-        made = [copy(x.at[rows, :], rowbuf.at[k, side], row_send.at[k, side], row_recv.at[k, side], a, to_r)
-                for k, x in enumerate((gs, rs))]
+        made = [copy(x.at[pl.ds(side * (h - n), n), :], rowbuf.at[k, side, pl.ds(side * (HALO - n), n), :],
+                     row_send.at[side], row_recv.at[side], a, to_r) for k, (x, n) in enumerate(((gs, HALO), (rs, HALO // 2)))]
         for p, to_a in ((0, al), (1, ar)):
             made.append(copy(pack.at[p, pl.ds(side * (fold - HALO), HALO), :], colbuf.at[p, pl.ds(fold + side * HALO, HALO), :],
-                             col_send.at[p, 1 + side], col_recv.at[p, 1 + side], to_a, to_r))
+                             col_send.at[1 + side], col_recv.at[1 + side], to_a, to_r))
         return made
+
+    def side_totals(side, to_r):
+        rows, corners = gs.at[pl.ds(0, HALO + HALO // 2), :], colbuf.at[0, pl.ds(0, 2 * HALO), :]
+        return [copy(rows, rows, row_send.at[side], row_recv.at[side], a, to_r),
+                copy(corners, corners, col_send.at[1 + side], col_recv.at[1 + side], a, to_r)]
 
     pl.semaphore_wait(barrier, na * (1 + (r > 0).astype(jnp.int32) + (r < nrad - 1).astype(jnp.int32)) - 1)
     for side in range(2):
@@ -277,10 +296,13 @@
         def _():
             for cp in row_copies(side)[2:]:
                 cp.start()
-    straight = [copy(pack.at[p], colbuf.at[p, pl.ds(0, fold), :], col_send.at[p, 0], col_recv.at[p, 0], to_a, r)
+    straight = [copy(pack.at[p], colbuf.at[p, pl.ds(0, fold), :], col_send.at[0], col_recv.at[0], to_a, r)
                 for p, to_a in ((0, al), (1, ar))]
+    straight_total = copy(pack, pack, col_send.at[0], col_recv.at[0], al, r)
     for cp in straight:
         cp.start()
+    for cp in loads[2]:
+        cp.wait()
     for side in range(2):
         @pl.when(ends[side])
         def _():
@@ -288,21 +310,16 @@
                 cp.start()
 
     spread = one_hot(256, 256, lambda c: 8 * (c % 32) + c // 32)
-    halo_spread = [one_hot(128, 1024, lambda c, k=k: jnp.where(
-        c % 128 < 2, 16 * k + 8 * (c % 128) + c // 128,
-        jnp.where(c % 128 >= 126, 32 + 16 * k + 8 * (c % 128 - 126) + c // 128, -1))) for k in range(2)]
+    halo_spread = one_hot(128, 256, lambda c: jnp.where(
+        (c + 2) % 16 < 8, -1, jnp.where((c + 2) % 16 >= 12, -1,
+                                        (c // 128) * 16 + (c % 128) // 16 + jnp.where(c % 16 >= 8, 8 * (c % 16 - 8), 8 * (c % 16 - 6) + 32))))
 
     def split_rows(x, count, put):
-        ln = lane((count, 128)) // 32
         for t in range(tiles):
             parts = [permute(x(slice((4 * t + b) * 256, (4 * t + b) * 256 + 256)), spread) for b in range(4)]
-            for gj in range(8):
-                o = None
-                for b in range(4):
-                    half = parts[b][:, (gj // 4) * 128:(gj // 4) * 128 + 128]
-                    piece = roll(half, 32 * (b - gj % 4), 1)
-                    o = piece if o is None else jnp.where(ln == b, piece, o)
-                put(gj, t, o)
+            for half in range(2):
+                for g, o in enumerate(transpose4([p[:, half * 128:half * 128 + 128] for p in parts])):
+                    put(4 * half + g, t, o)
 
     def put_own(k):
         def put(gj, t, value):
@@ -311,29 +328,39 @@
 
     for k, x in enumerate((gs, rs)):
         split_rows(lambda cols, x=x: x[:, cols], h, put_own(k))
-
-    for side in range(2):
-        @pl.when(ends[1 - side])
-        def _():
-            for cp in row_copies_in(side, rowbuf, colbuf, copy, row_send, row_recv, col_send, col_recv, gs, rs, pack, h, a, r):
-                cp.wait_recv()
-    for cp in straight:
-        cp.wait_recv()
-    announce(0)
-    at = (h, 8 * s0 - HALO)
+    for k, dst in enumerate((v0, g0)):
+        for gj in range(8):
+            for gi in range(8):
+                for t in range(tiles):
+                    dst[gi, gj, 0:blk, t * 128:t * 128 + 128] = stage[k, gj, t, pl.ds(gi, blk, stride=8), :]
     for k in range(2):
         for gj in range(8):
             for t in range(tiles + 1):
                 stage[k, gj, t, pl.ds(h + HALO, 8 * s0 - h - 2 * HALO), :] = jnp.zeros((8 * s0 - h - 2 * HALO, 128), F32)
+
+    for side in range(2):
+        @pl.when(ends[1 - side])
+        def _():
+            for cp in side_totals(side, r + 1 if side == 0 else r - 1):
+                cp.wait_recv()
+    straight_total.wait_recv()
+    announce(0)
+    at = (h, 8 * s0 - HALO)
     def put_edges(gj, t, value):
         for k in range(2):
             for side in range(2):
                 n = 2 * k + side
                 stage[k, gj, t, pl.ds(at[side], HALO), :] = value[n * HALO:(n + 1) * HALO]
 
-    split_rows(lambda cols: jnp.concatenate(
-        [jnp.where(ends[1 - side], rowbuf[k, side, :, cols], 0.0) for k in range(2) for side in range(2)], axis=0),
-        4 * HALO, put_edges)
+    def edge(k, side, cols):
+        if k == 0:
+            return [jnp.where(ends[1 - side], rowbuf[k, side, :, cols], 0.0)]
+        half = HALO // 2
+        x = jnp.where(ends[1 - side], rowbuf[k, side, side * half:side * half + half, cols], 0.0)
+        return [jnp.zeros_like(x), x] if side else [x, jnp.zeros_like(x)]
+
+    split_rows(lambda cols: jnp.concatenate(sum((edge(k, side, cols) for k in range(2) for side in range(2)), []), axis=0),
+               4 * HALO, put_edges)
 
     def beside(first, count, shift):
         right, left = colbuf[0, pl.ds(first, count), :], colbuf[1, pl.ds(first, count), :]
@@ -343,17 +370,18 @@
     strips.append(jnp.where(ends[1], beside(fold, HALO, 0), 0.0))
     strips.append(jnp.where(ends[0], beside(fold + HALO, HALO, 96), 0.0))
     strips = jnp.concatenate(strips, axis=0)
+    y = permute(strips, halo_spread)
     for k in range(2):
-        y = permute(strips, halo_spread[k])
         for gj in range(8):
-            cols = slice(gj * 128, gj * 128 + 128)
-            stage[k, gj, tiles, pl.ds(0, h + HALO), :] = y[0:h + HALO, cols]
-            stage[k, gj, tiles, pl.ds(at[1], HALO), :] = y[h + HALO:, cols]
+            piece = roll(y[:, k * 128:k * 128 + 128], -16 * gj - 8, 1)
+            stage[k, gj, tiles, pl.ds(0, h + HALO), :] = piece[0:h + HALO]
+            stage[k, gj, tiles, pl.ds(at[1], HALO), :] = piece[h + HALO:]
     for k, dst in enumerate((v0, g0)):
         for gj in range(8):
             for gi in range(8):
-                for t in range(tiles + 1):
-                    dst[gi, gj, :, t * 128:t * 128 + 128] = stage[k, gj, t, pl.ds(gi, s0, stride=8), :]
+                for t in range(tiles):
+                    dst[gi, gj, blk:s0, t * 128:t * 128 + 128] = stage[k, gj, t, pl.ds(h + gi, s0 - blk, stride=8), :]
+                dst[gi, gj, :, lanes:ext] = stage[k, gj, tiles, pl.ds(gi, s0, stride=8), :]
 
     fine = Grid(v0, g0, c0, 8, 8, False)
     middle = Grid(v1, g1, c1, 4, 4, False)
@@ -391,11 +419,16 @@
                      row1_send.at[side], row1_recv.at[side], a, to_r)]
         for p, to_a in ((0, al), (1, ar)):
             made.append(copy(s1.at[p, pl.ds(first, 8), :], q1.at[p, pl.ds(blk + 8 * side, 8), :],
-                             col1_send.at[p, 1 + side], col1_recv.at[p, 1 + side], to_a, to_r))
+                             col1_send.at[1 + side], col1_recv.at[1 + side], to_a, to_r))
         return made
 
-    straight1 = [copy(s1.at[p], q1.at[p, pl.ds(0, blk), :], col1_send.at[p, 0], col1_recv.at[p, 0], to_a, r)
+    def totals1(side, to_r):
+        corners = q1.at[0, pl.ds(0, 16), :]
+        return [copies1(side, to_r)[0], copy(corners, corners, col1_send.at[1 + side], col1_recv.at[1 + side], a, to_r)]
+
+    straight1 = [copy(s1.at[p], q1.at[p, pl.ds(0, blk), :], col1_send.at[0], col1_recv.at[0], to_a, r)
                  for p, to_a in ((0, al), (1, ar))]
+    straight1_total = copy(s1, s1, col1_send.at[0], col1_recv.at[0], al, r)
     for side in range(2):
         @pl.when(ends[side])
         def _():
@@ -415,10 +448,9 @@
     for side in range(2):
         @pl.when(ends[1 - side])
         def _():
-            for cp in copies1(side, r + 1 if side == 0 else r - 1):
+            for cp in totals1(side, r + 1 if side == 0 else r - 1):
                 cp.wait_recv()
-    for cp in straight1:
-        cp.wait_recv()
+    straight1_total.wait_recv()
     wl = lane((blk + 16, 128))
     sub = lax.broadcasted_iota(jnp.int32, (blk + 16, 128), 0)
     got = jnp.where(sub < blk, 1, jnp.where(sub < blk + 8, nrad - 1 - r, r)) > 0
@@ -437,29 +469,43 @@
     place = gat.at[a, pl.ds(pl.multiple_of(r * blk, 8), blk), :]
     gat[a, pl.ds(pl.multiple_of(r * blk, 8), blk), :] = wv[...]
 
-    def hand(da, dr):
-        step = da * nrad + dr
-        return copy(wv, place, all_send.at[step], all_recv.at[step], lax.rem(a + da, na), lax.rem(r + dr, nrad))
-
-    partner = r + 1 - 2 * lax.rem(r, 2)
-
-    def relay(da, dr):
-        step = da * nrad + dr + 1
-        came = gat.at[lax.rem(a + na - da, na), pl.ds(pl.multiple_of(lax.rem(r + nrad - dr, nrad) * blk, 8), blk), :]
-        return copy(came, came, all_send.at[step], all_recv.at[step], a, partner)
-
-    own = copy(wv, place, all_send.at[0], all_recv.at[0], a, partner)
+    z, core, nz = lax.div(r, 2), lax.rem(r, 2), nrad // 2
+
+    def hand(da, zt):
+        to_a = lax.rem(a + da, na)
+        return copy(wv, place, all_send, all_recv.at[a, z], to_a, 2 * zt + 1)
+
+    def relay(da, zs):
+        from_a = lax.rem(a + na - da, na)
+        came = gat.at[from_a, pl.ds(pl.multiple_of(2 * zs * blk, 8), 2 * blk), :]
+        return copy(came, came, relay_send.at[1 if da else 0], all_recv.at[from_a, zs], a, r + 1 - 2 * core)
+
+    own = copy(wv, place, all_send, all_recv.at[a, z], a, r + 1 - 2 * core)
+
+    def sent(ref, send):
+        copy(ref, ref, send, all_recv.at[0, 0], a, r + 1 - 2 * core).wait_send()
+
+    def each_chip(near_first, do):
+        for k in reversed(range(nz)) if near_first else range(nz):
+            zt = jnp.where(z < nz // 2, nz - 1 - k, k)
+            for da in reversed(range(na)):
+                if da:
+                    do(da, zt)
+                else:
+                    pl.when(zt != z)(lambda: do(0, zt))
+
+    def pass_on(da, zs):
+        relay(da, zs).wait_recv()
+        relay(da, zs).start()
+
     learn(len(reach) - 1)
-    for d in others:
-        hand(*d).start()
     own.start()
+    each_chip(False, lambda da, zt: hand(da, zt).start())
     load_table.wait()
-    for d in reversed(others):
-        hand(*d).wait_recv()
-        relay(*d).start()
+
+    pl.when(core == 1)(lambda: each_chip(True, pass_on))
+    pl.when(core == 0)(lambda: each_chip(True, lambda da, zs: relay(da, zs).wait_recv()))
     own.wait_recv()
-    for d in reversed(others):
-        relay(*d).wait_recv()
 
     w3 = lanes * na
     q3 = w3 // 4
@@ -469,7 +515,7 @@
     stacked = jnp.concatenate([jnp.concatenate(
         [rows3[t, pl.ds(gi, nrad, stride=16), :] for t in range(na * tiles)], axis=1) for gi in range(16)], axis=0)
     table3 = one_hot(w3, w3, lambda c: 4 * (c % q3) + c // q3)
-    by_group = permute(stacked, table3)
+    by_group = permute(stacked, table3, 2)
     for gi in range(16):
         for gj in range(4):
             b3[gi, gj] = by_group[gi * nrad:(gi + 1) * nrad, gj * q3:(gj + 1) * q3]
@@ -489,7 +535,7 @@
         nat5[gi] = value
     l4.restrict(t3, u3, put5)
     x5 = permute(jnp.concatenate([nat5[i] for i in range(4)], axis=0),
-                 one_hot(w5, 512, lambda c: 4 * (c % q5) + c // 128))
+                 one_hot(w5, 512, lambda c: 4 * (c % q5) + c // 128), 2)
     for gi in range(4):
         for gj in range(4):
             b5[gi, gj] = x5[gi * nrad:(gi + 1) * nrad, gj * 128:gj * 128 + 128]
@@ -553,55 +599,37 @@
     for side in range(2):
         @pl.when(ends[side])
         def _():
-            for cp in row_copies(side):
+            for cp in side_totals(side, r - 1 if side == 0 else r + 1):
                 cp.wait_send()
-    for cp in straight:
-        cp.wait_send()
+    straight_total.wait_send()
     for side in range(2):
         @pl.when(ends[side])
         def _():
-            for cp in copies1(side, r - 1 if side == 0 else r + 1):
+            for cp in totals1(side, r - 1 if side == 0 else r + 1):
                 cp.wait_send()
-    for cp in straight1:
-        cp.wait_send()
-    own.wait_send()
-    for d in others:
-        hand(*d).wait_send()
-        relay(*d).wait_send()
+    straight1_total.wait_send()
+    sent(gat.at[:, pl.ds(0, nz * blk), :], all_send)
+
+    @pl.when(core == 1)
+    def _():
+        sent(gat.at[pl.ds(0, na - 1)], relay_send.at[1])
+        sent(gat.at[0, pl.ds(0, (nz - 1) * 2 * blk), :], relay_send.at[0])
 
 
 def join_kernel(grouped_sol, grouped_res, sol, resid, whole, out_sem):
     tiles, h = grouped_sol.shape[1:3]
     join = one_hot(256, 256, lambda c: 32 * (c % 8) + c // 8)
-    ln = lax.broadcasted_iota(jnp.int32, (h, 128), 1) // 32
     copies = []
     for k, (x, out) in enumerate(((grouped_sol, sol), (grouped_res, resid))):
         for t in range(tiles):
+            halves = [transpose4([x[hf * 4 + p, t] for p in range(4)]) for hf in range(2)]
             for b in range(4):
-                halves = []
-                for hf in range(2):
-                    o = None
-                    for p in range(4):
-                        piece = roll(x[hf * 4 + p, t], 32 * (p - b), 1)
-                        o = piece if o is None else jnp.where(ln == p, piece, o)
-                    halves.append(o)
                 cols = pl.ds((4 * t + b) * 256, 256)
-                whole[k, :, cols] = permute(jnp.concatenate(halves, axis=1), join)
+                whole[k, :, cols] = permute(jnp.concatenate([halves[0][b], halves[1][b]], axis=1), join, 2)
                 copies.append(pltpu.make_async_copy(whole.at[k, :, cols], out.at[:, cols], out_sem.at[k, 4 * t + b]))
                 copies[-1].start()
     for cp in copies:
         cp.wait()
-
-
-def row_copies_in(side, rowbuf, colbuf, copy, row_send, row_recv, col_send, col_recv, gs, rs, pack, h, a, r):
-    rows = pl.ds(0, HALO)
-    to_r = r + 1 if side == 0 else r - 1
-    made = [copy(x.at[rows, :], rowbuf.at[k, side], row_send.at[k, side], row_recv.at[k, side], a, to_r)
-            for k, x in enumerate((gs, rs))]
-    for p in range(2):
-        made.append(copy(pack.at[p, rows, :], colbuf.at[p, pl.ds(h // 4 + side * HALO, HALO), :],
-                         col_send.at[p, 1 + side], col_recv.at[p, 1 + side], a, to_r))
-    return made
 
 
 def tmp_small(ref):
@@ -624,7 +652,7 @@
         table7 = pltpu.VMEM(table.shape, jnp.bfloat16)
         table = jnp.asarray(np.pad(table, ((0, 0), (0, max(0, 5 * h * w // table.shape[0] - table.shape[1])))))
         scratch = [
-            m(h, w), m(h, w), pltpu.SemaphoreType.DMA((2,)),
+            m(h, w), m(h, w), pltpu.SemaphoreType.DMA((2, 3)),
             m(2, 2, HALO, w), m(2, h // 4, 128), m(2, h // 4 + 2 * HALO, 128), m(2, blk, 128), m(2, blk + 16, 128), m(4, 4, 32, ext), m(4, 4, 32, ext),
             m(2, 8, tiles + 1, 8 * s0, 128),
             m(8, 8, s0, ext), m(8, 8, s0, ext), m(6, 8, s0, 128),
@@ -639,12 +667,9 @@
             m(2, 2, nrad, 128), m(2, 2, nrad, 128), m(6, 2, nrad, 128),
             m(1, 1, nrad, 128), m(1, 1, nrad, 128),
             m(16, 4, nrad, q3), m(8, 4, nrad, q3),
-            pltpu.SemaphoreType.DMA((2, 2)), pltpu.SemaphoreType.DMA((2, 2)),
-            pltpu.SemaphoreType.DMA((2, 3)), pltpu.SemaphoreType.DMA((2, 3)),
-            pltpu.SemaphoreType.DMA((2,)), pltpu.SemaphoreType.DMA((2,)),
-            pltpu.SemaphoreType.DMA((2, 3)), pltpu.SemaphoreType.DMA((2, 3)),
-            pltpu.SemaphoreType.DMA((na * nrad,)), pltpu.SemaphoreType.DMA((na * nrad,)),
-            pltpu.SemaphoreType.REGULAR((nrad.bit_length(), 2)),
+            *[pltpu.SemaphoreType.DMA((n,)) for n in (2, 2, 3, 3, 2, 2, 3, 3)],
+            pltpu.SemaphoreType.DMA, pltpu.SemaphoreType.DMA((na, nrad // 2)), pltpu.SemaphoreType.DMA((2,)),
+            pltpu.SemaphoreType.REGULAR((max(1, len([k for k in range(nrad.bit_length()) if 2 << k < nrad - 1])), 2)),
             table7, pltpu.SemaphoreType.DMA,
         ]
         grouped = pl.pallas_call(

time: 33.1 us -> 31.9 us (0.964)
  the two profiles are of different devices: /device:TPU:1 before, /device:TPU:0 now
where the time goes in v5:
time: 31.9 us; the launch traced here: 31.8 us
  Pallas kernels  31.1 us (97%)
  between operations  0.64 us (2%)
    pallas_call x1, Pallas kernels, local(): pl.pallas_call(lambda *refs: kernel(na, nrad, h, w, *refs), out_shape=[ja...  29.5 us
    pallas_call x1, Pallas kernels, local(): pl.pallas_call(join_kernel, out_shape=[jax.ShapeDtypeStruct((h, w), F32)]...  1.67 us

profile of v5, /device:TPU:0, one launch (start us, length us, event | category | flops | bytes accessed | tf_op | source)
XLA Modules:
  0.0 31.8 jit_solution(17961253783677554994)
XLA Ops:
  0.6 29.5 %shard_map.50 = (f32[8,1,128,128]{3,2,1,0:T(8,128)S(1)}, f32[8,1,128,128]{3,2,1,0:T(8,128)S(1)}) custom-call(f32[128,1024]{1,0:T(8,128)} %refs_0_.1, f32[128,1024]{1,0:T(8,128)} %refs_1_.1, bf16[256,2560]{1,0:T(8,128)(2,1)} %constant.2.clone.refs_2_), custom_call_target="tpu_custom_call" | custom-call | tf_op jit(solution)/shard_map/pallas_call | solution.py:675
  30.1 1.7 %shard_map.51 = (f32[128,1024]{1,0:T(8,128)}, f32[128,1024]{1,0:T(8,128)}) custom-call(f32[8,1,128,128]{3,2,1,0:T(8,128)S(1)} %get-tuple-element.4.grouped_sol, f32[8,1,128,128]{3,2,1,0:T(8,128)S(1)} %get-tuple-element.5.grouped_res), custom_call_target="tpu_custom_call" | custom-call | tf_op jit(solution)/shard_map/pallas_call | solution.py:683

commit v6 on v5

--- a/solution.py
+++ b/solution.py
@@ -123,18 +123,44 @@
     def coef(self, k, gi):
         return wide(self.c[k, gi], self.v.shape[-1])
 
+    def set_source(self, gi, gj, value):
+        self.g[gi, gj] = self.coef(0, gi) * value
+
     def update(self, gi, gj):
         v = self.v
-        return (self.coef(0, gi) * self.g[gi, gj] + self.coef(1, gi) * self.up(v, gi, gj)
+        return (self.g[gi, gj] + self.coef(1, gi) * self.up(v, gi, gj)
                 + self.coef(2, gi) * self.down(v, gi, gj)
                 + self.coef(3, gi) * (self.right(v, gi, gj) + self.left(v, gi, gj)))
+
+    def extent(self, gi, gj, depth, rows, cols):
+        near = lambda i, n: i < depth or i >= n - depth
+        return (self.v.shape[2] if near(gi, self.nr) else rows), (self.v.shape[3] if near(gj, self.nc) else cols)
+
+    def half_near(self, parity, depth, rows, cols):
+        for gi in range(self.nr):
+            for gj in range(self.nc):
+                if (gi + gj) % 2 == parity:
+                    m, n = self.extent(gi, gj, depth, rows, cols)
+                    self.v[gi, gj, 0:m, 0:n] = self.update(gi, gj)[0:m, 0:n]
+
+    def half_far(self, parity, depth, rows, cols):
+        full_m, full_n = self.v.shape[2:]
+        for gi in range(self.nr):
+            for gj in range(self.nc):
+                m, n = self.extent(gi, gj, depth, rows, cols)
+                if (gi + gj) % 2 == parity and (m < full_m or n < full_n):
+                    value = self.update(gi, gj)
+                    if m < full_m:
+                        self.v[gi, gj, m:full_m, :] = value[m:full_m]
+                    if n < full_n:
+                        self.v[gi, gj, 0:m, n:full_n] = value[0:m, n:full_n]
 
     def half(self, parity, first=False):
         for gi in range(self.nr):
             for gj in range(self.nc):
                 if (gi + gj) % 2 == parity:
                     if first:
-                        self.v[gi, gj] = self.coef(0, gi) * self.g[gi, gj]
+                        self.v[gi, gj] = self.g[gi, gj]
                     else:
                         self.v[gi, gj] = self.update(gi, gj)
 
@@ -144,27 +170,26 @@
             self.half(1)
             count -= 1
 
-        def body(_, carry):
+        for _ in range(count):
             self.half(0)
             self.half(1)
-            return carry
-
-        if count:
-            lax.fori_loop(0, count, body, 0)
-
-    def restrict(self, res, tmp, out):
+
+    def restrict(self, res, tmp, out, own=None):
         nr, nc = self.nr, self.nc
+        size = lambda gi, gj: self.extent(gi, gj, 1, *own) if own else self.v.shape[2:]
         for gi in range(nr):
             for gj in range(nc):
                 if (gi + gj) % 2 == 0:
-                    res[gi, gj] = self.coef(4, gi) * (self.update(gi, gj) - self.v[gi, gj])
+                    m, n = size(gi, gj)
+                    res[gi, gj, 0:m, 0:n] = (self.coef(4, gi) * (self.update(gi, gj) - self.v[gi, gj]))[0:m, 0:n]
         for big in range(nr // 2):
             for gj in range(nc):
                 if gj % 2 == 0:
                     a, b = 3.0 * res[2 * big, gj], self.up(res, 2 * big + 1, gj)
                 else:
                     a, b = 3.0 * res[2 * big + 1, gj], self.down(res, 2 * big, gj)
-                tmp[big, gj] = (a + b) * 0.125
+                m, n = own[0] if own else self.v.shape[2], size(0, gj)[1]
+                tmp[big, gj, 0:m, 0:n] = ((a + b) * 0.125)[0:m, 0:n]
         for big in range(nr // 2):
             for col in range(nc // 2):
                 inner = 3.0 * (tmp[big, 2 * col] + tmp[big, 2 * col + 1])
@@ -183,6 +208,8 @@
                 tmp[gi, col] = value
         for gi in range(self.nr):
             for gj in range(self.nc):
+                if (gi + gj) % 2 == 0:
+                    continue
                 near = tmp[gi, gj // 2]
                 far = coarse.left(tmp, gi, gj // 2) if gj % 2 == 0 else coarse.right(tmp, gi, gj // 2)
                 self.v[gi, gj] = self.v[gi, gj] + (0.75 * near + 0.25 * far)
@@ -321,6 +348,9 @@
                 for g, o in enumerate(transpose4([p[:, half * 128:half * 128 + 128] for p in parts])):
                     put(4 * half + g, t, o)
 
+    def scaled(k, gi, first, last, x):
+        return c0[0, gi, first:last] * x if k else x
+
     def put_own(k):
         def put(gj, t, value):
             stage[k, gj, t, pl.ds(0, h), :] = value
@@ -332,7 +362,7 @@
         for gj in range(8):
             for gi in range(8):
                 for t in range(tiles):
-                    dst[gi, gj, 0:blk, t * 128:t * 128 + 128] = stage[k, gj, t, pl.ds(gi, blk, stride=8), :]
+                    dst[gi, gj, 0:blk, t * 128:t * 128 + 128] = scaled(k, gi, 0, blk, stage[k, gj, t, pl.ds(gi, blk, stride=8), :])
     for k in range(2):
         for gj in range(8):
             for t in range(tiles + 1):
@@ -380,8 +410,8 @@
         for gj in range(8):
             for gi in range(8):
                 for t in range(tiles):
-                    dst[gi, gj, blk:s0, t * 128:t * 128 + 128] = stage[k, gj, t, pl.ds(h + gi, s0 - blk, stride=8), :]
-                dst[gi, gj, :, lanes:ext] = stage[k, gj, tiles, pl.ds(gi, s0, stride=8), :]
+                    dst[gi, gj, blk:s0, t * 128:t * 128 + 128] = scaled(k, gi, blk, s0, stage[k, gj, t, pl.ds(h + gi, s0 - blk, stride=8), :])
+                dst[gi, gj, :, lanes:ext] = scaled(k, gi, 0, s0, stage[k, gj, tiles, pl.ds(gi, s0, stride=8), :])
 
     fine = Grid(v0, g0, c0, 8, 8, False)
     middle = Grid(v1, g1, c1, 4, 4, False)
@@ -393,11 +423,12 @@
             ref[gi, gj] = value
         return put
 
-    fine.sweeps(PRE, False)
+    for step in range(2 * PRE):
+        fine.half_near(step % 2, 2 * PRE + 1 - step, blk, lanes)
 
     def put1(gi, gj, value):
-        g1[gi, gj, 0:blk, 0:lanes] = value[0:blk, 0:lanes]
-    fine.restrict(tmp_res, tmp_mid, put1)
+        g1[gi, gj, 0:blk, 0:lanes] = wide(c1[0, gi, 0:blk], lanes) * value[0:blk, 0:lanes]
+    fine.restrict(tmp_res, tmp_mid, put1, (blk, lanes))
 
     for side, first in ((0, blk), (1, blk + 8)):
         @pl.when(jnp.logical_not(ends[1 - side]))
@@ -459,7 +490,7 @@
         g1[g // 4, g % 4, :, lanes:ext] = jnp.where(
             wl < 8, roll(strip_r, -8 * g, 1), jnp.where(wl >= 120, roll(strip_l, 120 - 8 * g, 1), 0.0))
     middle.sweeps(PRE, True)
-    middle.restrict(t1, u1, into(g2))
+    middle.restrict(t1, u1, coarse.set_source)
     coarse.sweeps(PRE, True)
 
     def put3(gi, gj, value):
@@ -502,6 +533,8 @@
     own.start()
     each_chip(False, lambda da, zt: hand(da, zt).start())
     load_table.wait()
+    for step in range(2 * PRE):
+        fine.half_far(step % 2, 2 * PRE + 1 - step, blk, lanes)
 
     pl.when(core == 1)(lambda: each_chip(True, pass_on))
     pl.when(core == 0)(lambda: each_chip(True, lambda da, zs: relay(da, zs).wait_recv()))
@@ -518,14 +551,14 @@
     by_group = permute(stacked, table3, 2)
     for gi in range(16):
         for gj in range(4):
-            b3[gi, gj] = by_group[gi * nrad:(gi + 1) * nrad, gj * q3:(gj + 1) * q3]
+            b3[gi, gj] = wide(d3[0, gi], q3) * by_group[gi * nrad:(gi + 1) * nrad, gj * q3:(gj + 1) * q3]
 
     l3 = Grid(a3, b3, d3, 16, 4, True)
     l4 = Grid(a4, b4, d4, 8, 2, True)
     l5 = Grid(a5, b5, d5, 4, 4, True)
     l6 = Grid(a6, b6, d6, 2, 2, True)
     l3.sweeps(PRE, True)
-    l3.restrict(t3, u3, into(b4))
+    l3.restrict(t3, u3, l4.set_source)
     l4.sweeps(PRE, True)
     w5 = w3 // 4
     q5 = w5 // 4
@@ -538,9 +571,9 @@
                  one_hot(w5, 512, lambda c: 4 * (c % q5) + c // 128), 2)
     for gi in range(4):
         for gj in range(4):
-            b5[gi, gj] = x5[gi * nrad:(gi + 1) * nrad, gj * 128:gj * 128 + 128]
+            b5[gi, gj] = d5[0, gi] * x5[gi * nrad:(gi + 1) * nrad, gj * 128:gj * 128 + 128]
     l5.sweeps(PRE, True)
-    l5.restrict(tmp_small(t3), tmp_small(u3), into(b6))
+    l5.restrict(tmp_small(t3), tmp_small(u3), l6.set_source)
     l6.sweeps(PRE, True)
     l6.restrict(tmp_small(t3), tmp_small(u3), into(b7))
     a7[0, 0] = apply_operator(b7[0, 0], table7[...], w * na >> 7)
@@ -584,14 +617,12 @@
     near_end = lax.broadcasted_iota(jnp.int32, (8, ext), 0) < 4
     fine.add_prolonged(middle, tmp_res, True, lambda x: jnp.concatenate(
         [x[0:blk], jnp.where(near_end, x[blk:blk + 8], x[blk + 8:blk + 16])], axis=0))
-    fine.sweeps(POST, False)
+    for step in range(2 * POST):
+        fine.half_near(step % 2, 2 * POST - step, blk, lanes)
 
     for gi in range(8):
-        centre = fine.coef(4, gi)
-        out_c, in_c, ang_c = (fine.coef(k, gi) * centre for k in (1, 2, 3))
         for gj in range(8):
-            full = (g0[gi, gj] + out_c * fine.up(v0, gi, gj) + in_c * fine.down(v0, gi, gj)
-                    + ang_c * (fine.right(v0, gi, gj) + fine.left(v0, gi, gj)) - centre * v0[gi, gj])
+            full = fine.coef(4, gi) * (fine.update(gi, gj) - v0[gi, gj])
             for t in range(tiles):
                 cols = slice(t * 128, t * 128 + 128)
                 sol[gj, t, pl.ds(gi, blk, stride=8), :] = v0[gi, gj, 0:blk, cols]

time: 31.9 us -> 30.4 us (0.953)
  Pallas kernels: 31.1 us -> 29.6 us
    pallas_call x1, Pallas kernels: 29.5 us -> 27.9 us  [local(): pl.pallas_call(lambda *refs: kernel(na, nrad, h, w, *refs), out_shape=[ja...]
where the time goes in v6:
time: 30.4 us; the launch traced here: 30.2 us
  Pallas kernels  29.6 us (97%)
  between operations  0.64 us (2%)
    pallas_call x1, Pallas kernels, local(): pl.pallas_call(lambda *refs: kernel(na, nrad, h, w, *refs), out_shape=[ja...  27.9 us
    pallas_call x1, Pallas kernels, local(): pl.pallas_call(join_kernel, out_shape=[jax.ShapeDtypeStruct((h, w), F32)]...  1.68 us

profile of v6, /device:TPU:0, one launch (start us, length us, event | category | flops | bytes accessed | tf_op | source)
XLA Modules:
  0.0 30.2 jit_solution(15661904001296512781)
XLA Ops:
  0.6 27.9 %shard_map.50 = (f32[8,1,128,128]{3,2,1,0:T(8,128)S(1)}, f32[8,1,128,128]{3,2,1,0:T(8,128)S(1)}) custom-call(f32[128,1024]{1,0:T(8,128)} %refs_0_.1, f32[128,1024]{1,0:T(8,128)} %refs_1_.1, bf16[256,2560]{1,0:T(8,128)(2,1)} %constant.2.clone.refs_2_), custom_call_target="tpu_custom_call" | custom-call | tf_op jit(solution)/shard_map/pallas_call | solution.py:706
  28.6 1.7 %shard_map.51 = (f32[128,1024]{1,0:T(8,128)}, f32[128,1024]{1,0:T(8,128)}) custom-call(f32[8,1,128,128]{3,2,1,0:T(8,128)S(1)} %get-tuple-element.4.grouped_sol, f32[8,1,128,128]{3,2,1,0:T(8,128)S(1)} %get-tuple-element.5.grouped_res), custom_call_target="tpu_custom_call" | custom-call | tf_op jit(solution)/shard_map/pallas_call | solution.py:714

commit v7 on v6

--- a/solution.py
+++ b/solution.py
@@ -235,7 +235,8 @@
 def kernel(na, nrad, h, w, rs_in, gs_in, table_in, sol, resid, rs, gs, load_sem,
            rowbuf, pack, colbuf, s1, q1, t1, u1, stage, v0, g0, c0, v1, g1, c1, v2, g2, c2, v3, c3, wv, wg, tmp_res, tmp_mid,
            gat, rows3, nat3, a3, b3, d3, a4, b4, d4, a5, b5, d5, a6, b6, d6, a7, b7, t3, u3,
-           row_send, row_recv, col_send, col_recv, row1_send, row1_recv, col1_send, col1_recv, all_send, all_recv, relay_send, known, table7, table_sem):
+           row_send, row_recv, col_send, col_recv, row1_send, row1_recv, col1_send, col1_recv, all_send, all_recv, relay_send, known, table7, table_sem,
+           spread, halo_spread, split3, join3, split5, join5):
     a, r = lax.axis_index("ang"), lax.axis_index("rad")
     ar, al = lax.rem(a + 1, na), lax.rem(a + na - 1, na)
     lanes = w // 8
@@ -336,14 +337,15 @@
             for cp in row_copies(side)[:2]:
                 cp.start()
 
-    spread = one_hot(256, 256, lambda c: 8 * (c % 32) + c // 32)
-    halo_spread = one_hot(128, 256, lambda c: jnp.where(
+    spread[...] = one_hot(256, 256, lambda c: 8 * (c % 32) + c // 32)
+    halo_spread[...] = one_hot(128, 256, lambda c: jnp.where(
         (c + 2) % 16 < 8, -1, jnp.where((c + 2) % 16 >= 12, -1,
                                         (c // 128) * 16 + (c % 128) // 16 + jnp.where(c % 16 >= 8, 8 * (c % 16 - 8), 8 * (c % 16 - 6) + 32))))
 
     def split_rows(x, count, put):
         for t in range(tiles):
-            parts = [permute(x(slice((4 * t + b) * 256, (4 * t + b) * 256 + 256)), spread) for b in range(4)]
+            y = permute(jnp.concatenate([x(slice((4 * t + b) * 256, (4 * t + b) * 256 + 256)) for b in range(4)], axis=0), spread[...])
+            parts = [y[b * count:(b + 1) * count] for b in range(4)]
             for half in range(2):
                 for g, o in enumerate(transpose4([p[:, half * 128:half * 128 + 128] for p in parts])):
                     put(4 * half + g, t, o)
@@ -400,7 +402,7 @@
     strips.append(jnp.where(ends[1], beside(fold, HALO, 0), 0.0))
     strips.append(jnp.where(ends[0], beside(fold + HALO, HALO, 96), 0.0))
     strips = jnp.concatenate(strips, axis=0)
-    y = permute(strips, halo_spread)
+    y = permute(strips, halo_spread[...])
     for k in range(2):
         for gj in range(8):
             piece = roll(y[:, k * 128:k * 128 + 128], -16 * gj - 8, 1)
@@ -471,6 +473,14 @@
         @pl.when(ends[side])
         def _():
             copies1(side, r - 1 if side == 0 else r + 1)[0].start()
+    w3 = lanes * na
+    q3, w5 = w3 // 4, w3 // 4
+    q5 = w5 // 4
+    split3[...] = one_hot(w3, w3, lambda c: 4 * (c % q3) + c // q3)
+    join3[...] = one_hot(w3, w3, lambda c: (c % 4) * q3 + c // 4)
+    split5[...] = one_hot(w5, 512, lambda c: 4 * (c % q5) + c // 128)
+    for gj in range(4):
+        join5[gj] = one_hot(128, w5, lambda c, gj=gj: jnp.where(c % 4 == gj, c // 4, -1))
     learn(0)
     for k in range(1, len(reach)):
         announce(k)
@@ -540,15 +550,12 @@
     pl.when(core == 0)(lambda: each_chip(True, lambda da, zs: relay(da, zs).wait_recv()))
     own.wait_recv()
 
-    w3 = lanes * na
-    q3 = w3 // 4
     for aa in range(na):
         for t in range(tiles):
             rows3[aa * tiles + t] = gat[aa, :, t * 128:t * 128 + 128]
     stacked = jnp.concatenate([jnp.concatenate(
         [rows3[t, pl.ds(gi, nrad, stride=16), :] for t in range(na * tiles)], axis=1) for gi in range(16)], axis=0)
-    table3 = one_hot(w3, w3, lambda c: 4 * (c % q3) + c // q3)
-    by_group = permute(stacked, table3, 2)
+    by_group = permute(stacked, split3[...], 2)
     for gi in range(16):
         for gj in range(4):
             b3[gi, gj] = wide(d3[0, gi], q3) * by_group[gi * nrad:(gi + 1) * nrad, gj * q3:(gj + 1) * q3]
@@ -560,15 +567,13 @@
     l3.sweeps(PRE, True)
     l3.restrict(t3, u3, l4.set_source)
     l4.sweeps(PRE, True)
-    w5 = w3 // 4
-    q5 = w5 // 4
     nat5 = {}
 
     def put5(gi, gj, value):
         nat5[gi] = value
     l4.restrict(t3, u3, put5)
     x5 = permute(jnp.concatenate([nat5[i] for i in range(4)], axis=0),
-                 one_hot(w5, 512, lambda c: 4 * (c % q5) + c // 128), 2)
+                 split5[...], 2)
     for gi in range(4):
         for gj in range(4):
             b5[gi, gj] = d5[0, gi] * x5[gi * nrad:(gi + 1) * nrad, gj * 128:gj * 128 + 128]
@@ -586,7 +591,7 @@
     y5 = None
     for gj in range(4):
         x = jnp.concatenate([a5[gi, gj] for gi in range(4)], axis=0)
-        r0 = permute(x, one_hot(128, w5, lambda c, gj=gj: jnp.where(c % 4 == gj, c // 4, -1)))
+        r0 = permute(x, join5[gj])
         y5 = r0 if y5 is None else y5 + r0
     for gi in range(4):
         u3[gi, 0] = y5[gi * nrad:(gi + 1) * nrad]
@@ -604,7 +609,7 @@
     begin = pl.multiple_of(r * 16, 8)
     x3 = jnp.concatenate([nat3[t, pl.ds(begin, 32), :] for t in range(w3 // 128)], axis=1)
     x3 = jnp.concatenate([x3[8:24], x3[24:32], x3[0:8]], axis=0)
-    y3 = permute(x3, one_hot(w3, w3, lambda c: (c % 4) * q3 + c // 4))
+    y3 = permute(x3, join3[...])
     for aa in range(na):
         wg[aa] = y3[:, aa * lanes:(aa + 1) * lanes]
     v3[0, 0, :, 0:lanes] = wg[a]
@@ -702,6 +707,7 @@
             pltpu.SemaphoreType.DMA, pltpu.SemaphoreType.DMA((na, nrad // 2)), pltpu.SemaphoreType.DMA((2,)),
             pltpu.SemaphoreType.REGULAR((max(1, len([k for k in range(nrad.bit_length()) if 2 << k < nrad - 1])), 2)),
             table7, pltpu.SemaphoreType.DMA,
+            *[pltpu.VMEM(s, jnp.bfloat16) for s in ((256, 256), (128, 256), (w3, w3), (w3, w3), (q3, 512), (4, 128, q3))],
         ]
         grouped = pl.pallas_call(
             lambda *refs: kernel(na, nrad, h, w, *refs),

time: 30.4 us -> 30.3 us (level)
  no operation moved by 1% of the time
where the time goes in v7:
time: 30.3 us; the launch traced here: 30.2 us
  Pallas kernels  29.5 us (97%)
  between operations  0.64 us (2%)
    pallas_call x1, Pallas kernels, local(): pl.pallas_call(lambda *refs: kernel(na, nrad, h, w, *refs), out_shape=[ja...  27.8 us
    pallas_call x1, Pallas kernels, local(): pl.pallas_call(join_kernel, out_shape=[jax.ShapeDtypeStruct((h, w), F32)]...  1.68 us

profile of v7, /device:TPU:0, one launch (start us, length us, event | category | flops | bytes accessed | tf_op | source)
XLA Modules:
  0.0 30.2 jit_solution(12761593468876669000)
XLA Ops:
  0.6 27.8 %shard_map.50 = (f32[8,1,128,128]{3,2,1,0:T(8,128)S(1)}, f32[8,1,128,128]{3,2,1,0:T(8,128)S(1)}) custom-call(f32[128,1024]{1,0:T(8,128)} %refs_0_.1, f32[128,1024]{1,0:T(8,128)} %refs_1_.1, bf16[256,2560]{1,0:T(8,128)(2,1)} %constant.2.clone.refs_2_), custom_call_target="tpu_custom_call" | custom-call | tf_op jit(solution)/shard_map/pallas_call | solution.py:712
  28.5 1.7 %shard_map.51 = (f32[128,1024]{1,0:T(8,128)}, f32[128,1024]{1,0:T(8,128)}) custom-call(f32[8,1,128,128]{3,2,1,0:T(8,128)S(1)} %get-tuple-element.4.grouped_sol, f32[8,1,128,128]{3,2,1,0:T(8,128)S(1)} %get-tuple-element.5.grouped_res), custom_call_target="tpu_custom_call" | custom-call | tf_op jit(solution)/shard_map/pallas_call | solution.py:720

commit v8 on v7

--- a/solution.py
+++ b/solution.py
@@ -246,7 +246,7 @@
     lane = lambda shape: lax.broadcasted_iota(jnp.int32, shape, 1)
 
     spans = (pl.ds(0, 128), pl.ds(w - 128, 128), pl.ds(128, w - 256))
-    loads = [[pltpu.make_async_copy(src.at[:, cols], dst.at[:, cols], load_sem.at[k, n])
+    loads = [[pltpu.make_async_copy(src.at[:, cols], dst.at[:, cols], load_sem.at[k + 1 if n == 2 else 0])
               for k, (src, dst) in enumerate(((gs_in, gs), (rs_in, rs)))] for n, cols in enumerate(spans)]
     for cp in sum(loads, []):
         cp.start()
@@ -287,8 +287,7 @@
     for l, d, n in ((3, d3, 16), (4, d4, 8), (5, d5, 4), (6, d6, 2)):
         fill_coefficients(d, n, nrad, 0, (h * nrad) >> l, spacing[l], 0)
 
-    for cp in loads[0] + loads[1]:
-        cp.wait()
+    pltpu.make_async_copy(gs_in.at[:, 0:512], gs.at[:, 0:512], load_sem.at[0]).wait()
 
     fold = h // 4
     place16 = lane((fold, 128)) // 16
@@ -688,7 +687,7 @@
         table7 = pltpu.VMEM(table.shape, jnp.bfloat16)
         table = jnp.asarray(np.pad(table, ((0, 0), (0, max(0, 5 * h * w // table.shape[0] - table.shape[1])))))
         scratch = [
-            m(h, w), m(h, w), pltpu.SemaphoreType.DMA((2, 3)),
+            m(h, w), m(h, w), pltpu.SemaphoreType.DMA((3,)),
             m(2, 2, HALO, w), m(2, h // 4, 128), m(2, h // 4 + 2 * HALO, 128), m(2, blk, 128), m(2, blk + 16, 128), m(4, 4, 32, ext), m(4, 4, 32, ext),
             m(2, 8, tiles + 1, 8 * s0, 128),
             m(8, 8, s0, ext), m(8, 8, s0, ext), m(6, 8, s0, 128),

time: 30.3 us -> 30.3 us (level)
  no operation moved by 1% of the time
where the time goes in v8:
time: 30.3 us; the launch traced here: 30.1 us
  Pallas kernels  29.5 us (97%)
  between operations  0.64 us (2%)
    pallas_call x1, Pallas kernels, local(): pl.pallas_call(lambda *refs: kernel(na, nrad, h, w, *refs), out_shape=[ja...  27.8 us
    pallas_call x1, Pallas kernels, local(): pl.pallas_call(join_kernel, out_shape=[jax.ShapeDtypeStruct((h, w), F32)]...  1.68 us

profile of v8, /device:TPU:0, one launch (start us, length us, event | category | flops | bytes accessed | tf_op | source)
XLA Modules:
  0.0 30.1 jit_solution(11467770225189645135)
XLA Ops:
  0.6 27.8 %shard_map.50 = (f32[8,1,128,128]{3,2,1,0:T(8,128)S(1)}, f32[8,1,128,128]{3,2,1,0:T(8,128)S(1)}) custom-call(f32[128,1024]{1,0:T(8,128)} %refs_0_.1, f32[128,1024]{1,0:T(8,128)} %refs_1_.1, bf16[256,2560]{1,0:T(8,128)(2,1)} %constant.2.clone.refs_2_), custom_call_target="tpu_custom_call" | custom-call | tf_op jit(solution)/shard_map/pallas_call | solution.py:711
  28.5 1.7 %shard_map.51 = (f32[128,1024]{1,0:T(8,128)}, f32[128,1024]{1,0:T(8,128)}) custom-call(f32[8,1,128,128]{3,2,1,0:T(8,128)S(1)} %get-tuple-element.4.grouped_sol, f32[8,1,128,128]{3,2,1,0:T(8,128)S(1)} %get-tuple-element.5.grouped_res), custom_call_target="tpu_custom_call" | custom-call | tf_op jit(solution)/shard_map/pallas_call | solution.py:719
